TPU v7x, 128 devices: a whole 4x4x4 slice. The times are simulated.
128 devices in a mesh: batch: 1, col: 16 (over z, y), row: 8 (over x, core).
Axes of the slice: x: 4, y: 4, z: 4, core: 2. Of those that a mesh axis runs over, the one named last changes fastest.
Arguments:
- chol_fac: float32 [8192, 8192], P(('batch', 'row'), 'col')
- chol_bar: float32 [8192, 8192], P(('batch', 'row'), 'col')
Outputs:
- output: float32 [8192, 8192], P(('batch', 'row'), 'col')
All inputs are finite; a program needn't handle non-finite values.
Results may differ from a plain program's by a relative error of at most 0.001.
Values are sent between devices in bfloat16 or wider.
A program may use at most 1 GiB of HBM per device.

v0:
```python
import jax
import jax.numpy as jnp
from jax import lax
from jax.sharding import PartitionSpec as P

BLOCK_SIZE = 128
PREC_HIGH = lax.Precision.HIGHEST


def phi_part(matrix):
    idx_row = jnp.arange(matrix.shape[-2])[:, None]
    idx_col = jnp.arange(matrix.shape[-1])[None, :]
    return jnp.where(idx_row > idx_col, matrix, jnp.where(idx_row == idx_col, 0.5 * matrix, 0.0))


def diag_reverse(d_fac, d_bar):
    inner_mat = phi_part(jnp.einsum('ij,ik->jk', d_fac, d_bar, precision=PREC_HIGH, preferred_element_type=jnp.float32))
    left_solved = lax.linalg.triangular_solve(d_fac, inner_mat, left_side=True, lower=True, transpose_a=True)
    full_grad = lax.linalg.triangular_solve(d_fac, left_solved, left_side=False, lower=True)
    return phi_part(full_grad + full_grad.T)


def solution(mesh):
    row_devs = mesh.shape['row']
    col_devs = mesh.shape['col']

    def local_pass(chol_loc, bar_loc):
        rows_loc, cols_loc = chol_loc.shape
        total_blocks = (rows_loc // BLOCK_SIZE) * row_devs
        row_id = lax.axis_index('row')
        col_id = lax.axis_index('col')
        row_glob = (jnp.arange(rows_loc) // BLOCK_SIZE) * row_devs + row_id
        col_glob = (jnp.arange(cols_loc) // BLOCK_SIZE) * col_devs + col_id

        def block_step(step_num, work_mat):
            blk_idx = total_blocks - 1 - step_num
            on_row = row_id == blk_idx % row_devs
            on_col = col_id == blk_idx % col_devs
            row_off = (blk_idx // row_devs) * BLOCK_SIZE
            col_off = (blk_idx // col_devs) * BLOCK_SIZE
            below_mask = (row_glob > blk_idx)[:, None]
            left_mask = (col_glob < blk_idx)[None, :]
            d_here = lax.dynamic_slice(chol_loc, (row_off, col_off), (BLOCK_SIZE, BLOCK_SIZE))
            d_fac = lax.psum(jnp.where(on_row, d_here, 0.0), 'row')
            t_panel = lax.dynamic_slice(work_mat, (0, col_off), (rows_loc, BLOCK_SIZE))
            solved = lax.linalg.triangular_solve(d_fac, t_panel, left_side=False, lower=True)
            keep_solved = on_col & below_mask
            work_mat = lax.dynamic_update_slice(work_mat, jnp.where(keep_solved, solved, t_panel), (0, col_off))
            c_bar_all = lax.psum(jnp.where(keep_solved, solved, 0.0), 'col')
            l_row = lax.dynamic_slice(chol_loc, (row_off, 0), (BLOCK_SIZE, cols_loc))
            r_fac = lax.psum(jnp.where(on_row & left_mask, l_row, 0.0), 'row')
            work_mat = work_mat - jnp.dot(c_bar_all, r_fac, precision=PREC_HIGH, preferred_element_type=jnp.float32)
            cross_part = jnp.einsum('ri,rc->ic', c_bar_all, chol_loc, precision=PREC_HIGH, preferred_element_type=jnp.float32)
            cross_sum = lax.psum(cross_part, 'row')
            row_old = lax.dynamic_slice(work_mat, (row_off, 0), (BLOCK_SIZE, cols_loc))
            d_bar_old = lax.dynamic_slice(row_old, (0, col_off), (BLOCK_SIZE, BLOCK_SIZE))
            d_cross = lax.dynamic_slice(cross_sum, (0, col_off), (BLOCK_SIZE, BLOCK_SIZE))
            d_bar = diag_reverse(d_fac, jnp.tril(d_bar_old) - jnp.tril(d_cross))
            d_bar_all = lax.psum(jnp.where(on_col, d_bar, 0.0), 'col')
            row_new = row_old - jnp.where(left_mask, cross_sum, 0.0) - jnp.dot(d_bar_all + d_bar_all.T, r_fac, precision=PREC_HIGH, preferred_element_type=jnp.float32)
            diag_slot = lax.dynamic_slice(row_new, (0, col_off), (BLOCK_SIZE, BLOCK_SIZE))
            row_new = lax.dynamic_update_slice(row_new, jnp.where(on_col, d_bar, diag_slot), (0, col_off))
            return lax.dynamic_update_slice(work_mat, jnp.where(on_row, row_new, row_old), (row_off, 0))

        return lax.fori_loop(0, total_blocks, block_step, bar_loc)

    grid_spec = P(('batch', 'row'), 'col')
    return jax.shard_map(local_pass, mesh=mesh, in_specs=(grid_spec, grid_spec), out_specs=grid_spec, check_vma=False)
```

profile of v0, /device:TPU:1, one launch (start us, length us, event | category | flops | bytes accessed | tf_op | source)
XLA Modules:
  0.0 20022.5 jit_solution(9153577165157624507)
XLA Ops:
  8.1 20006.2 %while.18 = (s32[]{:T(128)}, f32[1024,512]{1,0:T(8,128)S(1)}, s32[]{:T(128)}, s32[]{:T(128)}, f32[1024,512]{1,0:T(8,128)}, /*index=5*/s32[]{:T(128)}, s32[]{:T(1...) while((s32[]{:T(128)}, f32[1024,512]{1,0:T(8,128)S(1)}, ...), condition=%wide.region_6.7_spmd.clone.clone, body=%wide.region_0.6_spmd.clone.clone.sunk | while | flops 1989969920 | bytes 26743780 | solution.py:65
  85.9 83.5 all-reduce.10.cloned.1.call-done
  711.0 83.5 all-reduce.10.cloned.1.call-done
  1023.8 83.5 all-reduce.10.cloned.1.call-done
  1648.9 83.5 all-reduce.10.cloned.1.call-done
  2274.3 83.5 all-reduce.10.cloned.1.call-done
  2899.1 83.5 all-reduce.10.cloned.1.call-done
  3211.9 83.5 all-reduce.10.cloned.1.call-done
  3524.3 83.5 all-reduce.10.cloned.1.call-done
  4461.8 83.5 all-reduce.10.cloned.1.call-done
  4774.5 83.5 all-reduce.10.cloned.1.call-done
  5087.3 83.5 all-reduce.10.cloned.1.call-done
  6025.1 83.5 all-reduce.10.cloned.1.call-done
  6337.9 83.5 all-reduce.10.cloned.1.call-done
  6650.6 83.5 all-reduce.10.cloned.1.call-done
  8525.5 83.5 all-reduce.10.cloned.1.call-done
  10400.8 83.5 all-reduce.10.cloned.1.call-done
  11338.6 83.5 all-reduce.10.cloned.1.call-done
  12901.4 83.5 all-reduce.10.cloned.1.call-done
  13213.9 83.5 all-reduce.10.cloned.1.call-done
  13838.7 83.5 all-reduce.10.cloned.1.call-done
  15088.8 83.5 all-reduce.10.cloned.1.call-done
  16651.4 83.5 all-reduce.10.cloned.1.call-done
  19152.1 83.5 all-reduce.10.cloned.1.call-done
  (2477 shorter events, 18071.1 us)
Async XLA Ops:
  9.6 159.7 all-reduce.10.cloned.1.call-start
  637.1 157.4 all-reduce.10.cloned.1.call-start
  949.9 157.4 all-reduce.10.cloned.1.call-start
  1575.0 157.4 all-reduce.10.cloned.1.call-start
  1887.7 157.4 all-reduce.10.cloned.1.call-start
  2200.4 157.4 all-reduce.10.cloned.1.call-start
  3137.9 157.4 all-reduce.10.cloned.1.call-start
  4387.8 157.4 all-reduce.10.cloned.1.call-start
  4700.6 157.4 all-reduce.10.cloned.1.call-start
  5013.4 157.4 all-reduce.10.cloned.1.call-start
  5326.1 157.4 all-reduce.10.cloned.1.call-start
  5951.2 157.4 all-reduce.10.cloned.1.call-start
  6263.9 157.4 all-reduce.10.cloned.1.call-start
  6576.7 157.4 all-reduce.10.cloned.1.call-start
  7826.8 157.4 all-reduce.10.cloned.1.call-start
  8764.3 157.4 all-reduce.10.cloned.1.call-start
  11264.7 157.4 all-reduce.10.cloned.1.call-start
  12515.1 157.4 all-reduce.10.cloned.1.call-start
  15014.9 157.4 all-reduce.10.cloned.1.call-start
  15952.4 157.4 all-reduce.10.cloned.1.call-start
  16577.5 157.4 all-reduce.10.cloned.1.call-start
  17515.0 157.4 all-reduce.10.cloned.1.call-start
  18140.4 157.4 all-reduce.10.cloned.1.call-start
  19703.2 157.4 all-reduce.10.cloned.1.call-start
  (490 other events, 39359.0 us)
Sparse Core Ops, SparseCore 0:
  84.3 85.0 all-reduce.9
  709.4 85.0 all-reduce.9
  1022.1 85.0 all-reduce.9
  1334.6 85.0 all-reduce.9
  1647.2 85.0 all-reduce.9
  2272.7 85.0 all-reduce.9
  2897.5 85.0 all-reduce.9
  3210.2 85.0 all-reduce.9
  3522.7 85.0 all-reduce.9
  4460.1 85.0 all-reduce.9
  4772.9 85.0 all-reduce.9
  5085.6 85.0 all-reduce.9
  5398.3 85.0 all-reduce.9
  6023.5 85.0 all-reduce.9
  6336.2 85.0 all-reduce.9
  6649.0 85.0 all-reduce.9
  8211.5 85.0 all-reduce.9
  8523.9 85.0 all-reduce.9
  10399.2 85.0 all-reduce.9
  11337.0 85.0 all-reduce.9
  13837.0 85.0 all-reduce.9
  15087.2 85.0 all-reduce.9
  16649.8 85.0 all-reduce.9
  19150.5 85.0 all-reduce.9
  (232 shorter events, 16234.6 us)
where the time goes:
time: 20000 us
  waiting for transfers between devices  18300 us (92%)
  other arithmetic  1000 us (5%)
  matrix products  619 us (3%)
    psum x64, waiting for transfers between devices, block_step(): c_bar_all = lax.psum(jnp.where(keep_solved, solved, 0.0), 'col')  5340 us
    psum x64, waiting for transfers between devices, block_step(): d_bar_all = lax.psum(jnp.where(on_col, d_bar, 0.0), 'col')  5290 us
    psum x64, waiting for transfers between devices, block_step(): r_fac = lax.psum(jnp.where(on_row & left_mask, l_row, 0.0), 'row')  3840 us
    psum x64, waiting for transfers between devices, block_step(): d_fac = lax.psum(jnp.where(on_row, d_here, 0.0), 'row')  3820 us
    another operation x128, other arithmetic, block_step(): lax.linalg.triangular_solve(d_fac, t_panel, left_side=False, lower=True)  682 us
  transfers between devices with their start and end apart: 256, of which 256 were waited for; matrix products, arithmetic and copies ran while one was open for 1% of the time, Pallas kernels for 0%

commit v1 on v0

v1 whole, which is shorter than its diff:
```python
import jax
import jax.numpy as jnp
from jax import lax
from jax.experimental import pallas as pl
from jax.experimental.pallas import tpu as pltpu
from jax.sharding import PartitionSpec as P

B, Q, H, K, N = 128, 256, 512, 1024, 2048
U, R = 4, 8
GROUPS = tuple(range(U))
OFF = tuple(K * u - B * u * (u - 1) for u in GROUPS)
ROWS = OFF[-1] + Q
HI = lax.Precision.HIGHEST
MESH = pl.DeviceIdType.MESH
VM = pl.BlockSpec(memory_space=pltpu.VMEM)
HB = pl.BlockSpec(memory_space=pl.ANY)
ALL = slice(None)


def mm(a, b):
    return jnp.dot(a, b, precision=HI, preferred_element_type=jnp.float32)


def mm_t(a, b):
    return lax.dot_general(a, b, (((0,), (0,)), ((), ())), precision=HI, preferred_element_type=jnp.float32)


def mod4(v):
    return lax.rem(v + U, U)


def at(start, size=B):
    return pl.ds(start if isinstance(start, int) else pl.multiple_of(start, B), size)


def group(u):
    return slice(OFF[u], OFF[u] + K - Q * u)


def wide(ref, rows, zs=GROUPS):
    return jnp.concatenate([ref[z, rows] for z in zs], axis=1)


def phi(block, ahead):
    diff = B * ahead + lax.broadcasted_iota(jnp.int32, (B, B), 0) - lax.broadcasted_iota(jnp.int32, (B, B), 1)
    return jnp.where(diff > 0, block, jnp.where(diff == 0, 0.5 * block, 0.0))


def step(g):
    return next(g, g) is not g


def run(*gathers, behind=()):
    live = list(gathers)
    while live:
        live = [g for g in live if step(g)]
        for g in behind:
            step(g)


def chain(*gathers):
    for g in gathers:
        step(g)
        yield


class Net:
    def __init__(self, send_sems, recv_sems):
        self.send_sems, self.recv_sems = send_sems, recv_sems
        self.r, self.c = lax.axis_index('row'), lax.axis_index('col')
        self.x, self.core = self.r // 2, lax.rem(self.r, 2)
        self.z, self.y = self.c // U, lax.rem(self.c, U)
        self.right, self.left = self.device(x=mod4(self.x + 1)), self.device(x=mod4(self.x - 1))
        self.partner = self.device(core=1 - self.core)
        self.zy = [self.device(y=mod4(self.y + 1)), self.device(y=mod4(self.y - 1)),
                   self.device(z=mod4(self.z + 1)), self.device(z=mod4(self.z - 1))]
        self.far_z = self.device(z=mod4(self.z + 2))
        self.copies = []

    def device(self, **place):
        x, core, y, z = [place.get(k, getattr(self, k)) for k in ('x', 'core', 'y', 'z')]
        return {'col': U * z + y, 'row': 2 * x + core}

    def barrier(self, *peers):
        sem = pltpu.get_barrier_semaphore()
        for peer in peers:
            pl.semaphore_signal(sem, inc=1, device_id=peer, device_id_type=MESH)
        pl.semaphore_wait(sem, len(peers))

    def line(self):
        places = [(mod4(self.x + d // 2), lax.rem(self.core + d, 2)) for d in range(1, R)]
        return [(self.device(x=x, core=core), 2 * x + core) for x, core in places]

    def plane(self):
        places = [(mod4(self.z + d // U), mod4(self.y + d % U)) for d in range(1, U * U)]
        return [(self.device(z=z, y=y), U * z + y) for z, y in places]

    def copy(self, ref, peer, dst=None):
        k = len(self.copies)
        copy = pltpu.make_async_remote_copy(
            src_ref=ref, dst_ref=ref if dst is None else dst, send_sem=self.send_sems.at[k], recv_sem=self.recv_sems.at[k],
            device_id=peer, device_id_type=MESH)
        copy.start()
        self.copies.append(copy)
        return copy

    def drain(self):
        for copy in self.copies:
            copy.wait_send()

    def gather_x(self, ref, axis=1, first=0):
        half = ref.shape[1 - axis] // 2

        def view(r, part=None):
            other = ALL if part is None else pl.ds(part * half, half)
            return ref.at[(other, first + r) if axis else (r, other)]

        near_r, near_l, far = [2 * mod4(self.x + d) + self.core for d in (1, -1, 2)]
        to_right, to_left = self.copy(view(self.r), self.right), self.copy(view(self.r), self.left)
        over = [self.copy(view(self.r), self.partner)]
        yield
        to_right.wait_recv()
        far_0 = self.copy(view(near_l, 0), self.right)
        over.append(self.copy(view(near_l), self.partner))
        to_left.wait_recv()
        far_1 = self.copy(view(near_r, 1), self.left)
        over.append(self.copy(view(near_r), self.partner))
        yield
        far_0.wait_recv()
        over.append(self.copy(view(far, 0), self.partner))
        far_1.wait_recv()
        over.append(self.copy(view(far, 1), self.partner))
        yield
        for copy in over:
            copy.wait_recv()
        yield

    def gather_zy(self, ref, start, count):
        yp, ym, zp, zm = self.zy
        y, z, n = self.y, self.z, count // U
        y_m, y_p, z_m, z_p = mod4(y - 1), mod4(y + 1), mod4(z - 1), mod4(z + 1)

        def view(zs, part, ys=None, parts=1):
            return ref.at[zs, pl.ds(start + part * n, parts * n), ALL if ys is None else at(B * ys)]

        def both(first, second, to_first, to_second):
            return self.copy(first, to_first), self.copy(second, to_second)

        a = both(view(z, 0, y, 2), view(z, 0, y, 2), yp, ym)
        b = both(view(z, 2, y, 2), view(z, 2, y, 2), zp, zm)
        yield
        for copy in a:
            copy.wait_recv()
        a = both(view(z, 0, y_m), view(z, 1, y_p), yp, ym)
        for copy in b:
            copy.wait_recv()
        b = both(view(z_m, 2, y), view(z_p, 3, y), zp, zm)
        yield
        for copy in a:
            copy.wait_recv()
        a = both(view(z, 0, None, 2), view(z, 0, None, 2), zp, zm)
        for copy in b:
            copy.wait_recv()
        b = both(view(ALL, 2, y, 2), view(ALL, 2, y, 2), yp, ym)
        yield
        for copy in a:
            copy.wait_recv()
        a = both(view(z_m, 0), view(z_p, 1), zp, zm)
        for copy in b:
            copy.wait_recv()
        b = both(view(ALL, 2, y_m), view(ALL, 3, y_p), yp, ym)
        yield
        for copy in (*a, *b):
            copy.wait_recv()
        yield

    def gather_y(self, ref, start, count):
        half, y = count // 2, self.y
        yp, ym = self.zy[:2]

        def view(ys, part=None):
            return ref.at[pl.ds(start, count) if part is None else pl.ds(start + part * half, half), at(B * ys)]

        near = self.copy(view(y), yp), self.copy(view(y), ym)
        yield
        near[0].wait_recv()
        far_0 = self.copy(view(mod4(y - 1), 0), yp)
        near[1].wait_recv()
        far_1 = self.copy(view(mod4(y + 1), 1), ym)
        yield
        far_0.wait_recv()
        far_1.wait_recv()
        yield

    def spread_z(self, *parts):
        sent = []
        for d, peer in ((1, self.zy[2]), (-1, self.zy[3]), (2, self.far_z)):
            for src, dst in parts:
                sent.append((self.copy(src(mod4(self.z + d)), peer, dst(self.z)), dst(mod4(self.z - d))))
        yield
        over = []
        for copy, got in sent:
            copy.wait_recv()
            over.append(self.copy(got, self.partner))
        yield
        for copy in over:
            copy.wait_recv()
        yield

    def transpose(self, a, b, d, out):
        def on_line(k):
            return ALL, k

        def on_plane(k):
            return k // R, lax.rem(k, R)

        line, plane = (self.line(), self.r, on_line), (self.plane(), self.c, on_plane)
        for src, dst, (others, me, piece) in ((a, b, line), (b, d, plane), (d, out, line)):
            sent = [self.copy(src.at[piece(place)], peer, dst.at[piece(me)]) for peer, place in others]
            dst[piece(me)] = src[piece(me)]
            yield
            for copy in sent:
                copy.wait_recv()
        yield

    def reduce(self, acc, fwd, end, start, count, put, terms=None, width=None):
        half, lanes = count // 2, ALL if width is None else pl.ds(0, width)
        rows, lo, hi, mid = pl.ds(start, count), pl.ds(start, half), pl.ds(start + half, half), pl.ds(start // 2, half)
        me, right, left = (self.z, *self.zy[2:]) if terms is None else (self.x, self.right, self.left)
        far, nxt, prv = [mod4(me + d) for d in (2, 1, -1)]
        if terms is not None:
            over = self.copy(terms.at[:, 1 - self.core, rows, lanes], self.partner, acc.at[:, rows, lanes])
            yield
            over.wait_recv()

        def settle(k):
            if terms is not None:
                acc[k, rows, lanes] = acc[k, rows, lanes] + terms[k, self.core, rows, lanes]

        def send(k, part, to, ref, slot):
            return self.copy(acc.at[k, part, lanes], to, ref.at[slot, mid, lanes])

        settle(far)
        far_r, far_l = send(far, lo, right, fwd, 0), send(far, hi, left, fwd, 1)
        settle(nxt)
        settle(prv)
        last = [send(nxt, hi, right, end, 0), send(prv, lo, left, end, 1)]
        settle(me)
        yield
        far_r.wait_recv()
        acc[nxt, lo, lanes] = acc[nxt, lo, lanes] + fwd[0, mid, lanes]
        last.append(send(nxt, lo, right, end, 2))
        far_l.wait_recv()
        acc[prv, hi, lanes] = acc[prv, hi, lanes] + fwd[1, mid, lanes]
        last.append(send(prv, hi, left, end, 3))
        yield
        for copy in last:
            copy.wait_recv()
        blocks = count // B
        for k in range(blocks):
            one, two = (1, 2) if 2 * k < blocks else (0, 3)
            row = pl.ds(start // 2 + B * (k % (blocks // 2)), B)
            put(k, acc[me, pl.ds(start + B * k, B), lanes] + (end[one, row, lanes] + end[two, row, lanes]))
        yield


def invert(w_ref, l_ref, tmp_ref):
    row = lax.broadcasted_iota(jnp.int32, (Q, Q), 0)
    col = lax.broadcasted_iota(jnp.int32, (Q, Q), 1)
    w_ref[...] = jnp.zeros_like(w_ref)

    def block(ref, i, j, size):
        return ref[i // B:(i + size) // B, :, j:j + size].reshape(size, size)

    def put(i, j, size, val):
        w_ref[i // B:(i + size) // B, :, j:j + size] = val.reshape(size // B, B, size)

    corners = range(0, K, Q)
    for k in corners:
        a = block(l_ref, k, k, Q)
        diag = jnp.where(row == col, a, 0.0)
        down, across = 1.0 / jnp.sum(diag, axis=1, keepdims=True), 1.0 / jnp.sum(diag, axis=0, keepdims=True)
        low = (row // 2 == col // 2) & (row > col)
        put(k, k, Q, jnp.where(row == col, down, jnp.where(low, -a * down * across, 0.0)))
    size = 2
    while size < Q:
        pair = (row // (2 * size) == col // (2 * size)) & (row // size > col // size)
        for k in corners:
            tmp_ref[k // Q] = mm(jnp.where(pair, block(l_ref, k, k, Q), 0.0), block(w_ref, k, k, Q))
        yield
        for k in corners:
            w = block(w_ref, k, k, Q)
            put(k, k, Q, w - mm(w, tmp_ref[k // Q]))
        yield
        size *= 2
    while size < K:
        for j in range(0, K, 2 * size):
            i = j + size
            part = mm(block(l_ref, i, j, size), block(w_ref, j, j, size))
            put(i, j, size, -mm(block(w_ref, i, i, size), part))
            yield
        size *= 2


def inner(net, u, start, panel, top, bar, terms):
    def two(k, _):
        h, x = k // U, lax.rem(k, U)
        p = mm_t(panel[2 * h + x // 2, top:top + K - Q * u, at(Q * lax.rem(x, 2), Q)], bar[Q * u:, :B * (u + 1)])
        for e in range(2):
            for v in range(u + 1):
                val = p[B * e:B * (e + 1), B * v:B * (v + 1)]
                terms[x, e, at(start + Q * v + B * h), :] = phi(val, 2 * k + e - net.c) if v == u else val
        return 0

    lax.fori_loop(0, R, two, 0)


def front_kernel(l_ref, bar_ref, lr_ref, col_ref, s_ref, lv, lss, wss, tmp, terms, acc, fwd, end, dma_sems, send_sems, recv_sems):
    net = Net(send_sems, recv_sems)
    r, c, y, z, core = net.r, net.c, net.y, net.z, net.core
    half, zz = z // 2, lax.rem(z, 2)
    ways = (1, 2, 3)
    others = [net.device(y=mod4(y + d)) for d in ways]
    net.barrier(net.right, net.left, net.partner, *others, *net.zy[2:])

    strip = at(B * (U * zz + y))

    def own(u):
        return at(B * (2 * u + half)), at(B * u)

    sent = [net.copy(l_ref.at[own(mod4(y + d))], other, lss.at[r, :, strip]) for d, other in zip(ways, others)]
    lss[r, :, strip] = l_ref[own(y)]
    for u in GROUPS:
        lv[z, group(u), at(B * y)] = l_ref[Q * u:, B * u:B * (u + 1)]
    g = [net.gather_zy(lv, OFF[u], K - Q * u) for u in GROUPS]
    run(chain(g[3], g[2]))
    for copy in sent:
        copy.wait_recv()
    pair = net.copy(lss.at[r, :, at(H * zz, H)], net.device(z=2 * half + 1 - zz))
    run(chain(g[1], g[0], g[3], g[3]))
    pair.wait_recv()

    order = iter([2, 2, 3, 1, 3, 2, 1, 2, 0, 1, 0, 1, 0, 0])
    stores = []

    def tick():
        u = next(order, None)
        if u is not None:
            step(g[u])

    def keep(u):
        stores.append(pltpu.make_async_copy(lv.at[:, group(u)], lr_ref.at[:, group(u)], dma_sems.at[u]))
        stores[-1].start()

    def begin(u):
        start = ROWS - Q * (u + 1) * (u + 2) // 2
        inner(net, u, start, lv, OFF[u], bar_ref, terms)

        def put(k, val):
            v, h = k // 2, k % 2
            s_ref[h, B * (u * (u + 1) // 2 + v):B * (u * (u + 1) // 2 + v + 1), :] = val

        keep(u)
        return net.reduce(acc, fwd, end, start, Q * (u + 1), put, terms)

    strips = net.gather_x(lss, axis=0)
    step(strips)
    for _ in range(3):
        tick()
    step(strips)
    for _ in range(2):
        tick()
    step(strips)
    s3 = begin(3)
    run(strips)
    step(s3)
    for k, _ in enumerate(invert(wss, lss, tmp)):
        if k % 4 == 1:
            tick()
        if k % 6 == 5:
            step(s3)
    s2 = begin(2)
    step(s2)
    tick()

    mine = pl.ds(U * core, U)
    sent = [net.copy(wss.at[mine, :, at(B * (U * zz + mod4(y + d)))], other, col_ref.at[y, mine]) for d, other in zip(ways, others)]
    col_ref[y] = wss[:, :, strip]
    step(s2)
    tick()
    tick()
    s1 = begin(1)
    run(s3, s2)
    over = []
    for d, copy in zip(ways, sent):
        copy.wait_recv()
        over.append(net.copy(col_ref.at[mod4(y - d), mine], net.partner))
    run(s1)
    for _ in range(U):
        tick()
    keep(0)
    for copy in over:
        copy.wait_recv()
    for copy in stores:
        copy.wait()
    net.drain()


def levels_kernel(lr_ref, bar_ref, wc_ref, s_ref, sy_ref, w_ref, row_e, row_d, row_o, col_3,
                  own, a, b, d, back, la, lb, l0, l1, bv, cd, re, rd, co, ro, c3, x1, x2, x3, terms, acc, fwd, end, dma_sems, send_sems, recv_sems):
    net = Net(send_sems, recv_sems)
    r, c, y, z = net.r, net.c, net.y, net.z
    sems = iter(range(32))

    def local(a, b):
        copy = pltpu.make_async_copy(a, b, dma_sems.at[next(sems)])
        copy.start()
        return copy

    load_s = local(s_ref, a)
    load_0 = [local(lr_ref.at[:, group(0)], l0), local(bar_ref.at[:, 0:B], bv)]
    load_a = [local(lr_ref.at[0:2, OFF[u] + B:OFF[u] + Q], la.at[:, B * u:B * (u + 1)]) for u in GROUPS]
    load_b = [local(lr_ref.at[:, OFF[u] + Q:OFF[u] + H], lb.at[:, B * u:B * (u + 2)]) for u in (0, 2)]
    load_c = local(lr_ref.at[:, OFF[1] + Q:OFF[2]], l1)
    net.barrier(*[peer for peer, _ in net.line() + net.plane()])
    piece = a.shape[2]

    def block(ref, k, u, v):
        top = B * (u * (u + 1) // 2 + v)
        i, low = top // piece, top % piece
        first = ref[k, i, low:low + B]
        return first if low + B <= piece else jnp.concatenate([first, ref[k, i + 1, :low + B - piece]], axis=0)

    low = c < R
    stores = []
    for u in GROUPS:
        re[z, B * u:B * (u + 1), at(B * y)] = wc_ref[u, r]
    diag = net.gather_zy(re, 0, H)
    step(diag)
    load_s.wait()
    for u in range(1, U):
        for h in range(2):
            for v in range(u + 1):
                own[v, B * (2 * u + h):B * (2 * u + h + 1), :] = block(a, h, u, v)
    places = [local(own.at[v, Q * (v + 1):], sy_ref.at[K * v + Q * (v + 1):K * (v + 1), at(B * y)]) for v in range(U - 1)]
    for place in places:
        place.wait()
    early = [net.gather_y(sy_ref, K * v + Q * (v + 1), K - Q * (v + 1)) for v in range(U - 1)]
    late = [net.gather_y(sy_ref, K * v, Q * (v + 1)) for v in GROUPS]
    moves = chain(*[early[k] for k in (0, 1, 0, 2, 1, 0, 2, 1, 2)])
    half = pl.ds(2 * net.core, 2)
    step(moves)

    for u in GROUPS:
        load_a[u].wait()
        cd[u, 0:R] = jnp.where(low, wc_ref[u], 0.0)
        x1[u, r] = mm(wide(la, slice(B * u, B * (u + 1)), (0, 1)), cd[u, 0:R].reshape(K, B))
    strips = net.gather_x(x1)
    step(strips)
    for load in load_0:
        load.wait()
    inner(net, 0, 0, l0, 0, bv, terms)

    def put(k, val):
        a[k, 0, :B] = val

    run(strips, net.reduce(acc, fwd, end, 0, Q, put, terms), diag)
    flip = net.transpose(a, b, d, back)
    step(flip)
    stores.append(local(re, row_e))
    for u in GROUPS:
        w = -mm(wide(re, slice(B * u, B * (u + 1)), (2, 3)), x1[u].reshape(K, B))
        w = jnp.where(low, w, wc_ref[u, r])
        cd[u, R + r] = w
        rd[z, B * u:B * (u + 1), at(B * y)] = w
    rows = net.gather_zy(rd, 0, H)
    step(rows)
    run(net.gather_x(cd, first=R), behind=[rows, moves])
    stores.append(local(cd.at[:, pl.ds(U * z, U)], w_ref.at[0:U, z]))
    out = net.spread_z((lambda k: cd.at[:, pl.ds(U * k + 2 * net.core, 2)], lambda k: w_ref.at[0:U, k, half]))
    step(out)
    moves = chain(moves, moves, moves, out, out)
    step(flip)

    for q in range(2):
        load_b[q].wait()
        x2[2 * q:2 * q + 2, r] = mm(wide(lb, slice(Q * q, Q * (q + 1))), cd[2 * q].reshape(N, B)).reshape(2, B, B)
    run(net.gather_x(x2), rows, behind=[moves])
    step(flip)
    stores.append(local(rd, row_d))
    for q in range(2):
        at_u = slice(B * (2 * q + 1), B * (2 * q + 2))
        tops = (mm(wide(re, at_u, (0, 1)), x2[2 * q].reshape(K, B)), mm(wide(rd, at_u), x2[2 * q:2 * q + 2].reshape(N, B)))
        for i, w in enumerate(tops):
            co[2 * q + i, r] = -w
            ro[z, B * (2 * q + i):B * (2 * q + i + 1), at(B * y)] = -w
    rows = net.gather_zy(ro, 0, H)
    step(rows)
    run(net.gather_x(co), behind=[rows, moves])
    run(moves)
    parts = []
    for q in range(2):
        stores.append(local(co.at[2 * q + z // 2, pl.ds(U * lax.rem(z, 2), U)], w_ref.at[U + q, z]))
        parts.append((lambda k, q=q: co.at[2 * q + k // 2, pl.ds(U * lax.rem(k, 2) + 2 * net.core, 2)],
                      lambda k, q=q: w_ref.at[U + q, k, half]))
    out = net.spread_z(*parts)
    step(out)

    load_c.wait()
    x3[:, r] = mm(wide(l1, ALL), jnp.concatenate([co[0:2].reshape(N, B), cd[1].reshape(N, B)], 1)).reshape(U, B, Q)
    x3[:, r, :, :B] = x3[:, r, :, :B] + mm(wide(l0, slice(H, K)), cd[0].reshape(N, B)).reshape(U, B, B)
    strips = net.gather_x(x3)
    step(strips)

    step(flip)
    for h in range(2):
        own[0, B * h:B * (h + 1), :] = block(a, h, 0, 0)
    for s in range(2):
        for u in GROUPS:
            for v in range(u + 1):
                at_t = slice(B * (2 * v + s), B * (2 * v + s + 1))
                val = block(back, s, u, v).T
                own[u, at_t, :] = own[u, at_t, :] + val if u == v else val
    places = [local(own.at[v, 0:Q * (v + 1)], sy_ref.at[K * v:K * v + Q * (v + 1), at(B * y)]) for v in GROUPS]
    run(strips, rows)
    for place in places:
        place.wait()
    moves = chain(*[late[k] for k in (3, 2, 3, 1, 2, 3, 0, 1, 2, 0, 1, 0)])
    step(moves)
    step(moves)
    stores.append(local(ro, row_o))
    for i in GROUPS:
        u = 2 + i // 2
        at_u = slice(B * u, B * (u + 1))
        if i % 2 == 0:
            w = mm(wide(re, at_u, (0, 1)), x3[i].reshape(K, Q))
        else:
            w = mm(wide(rd, at_u), x3[i - 1:i + 1].reshape(N, Q))
        if i >= 2:
            w = w + mm(wide(ro, slice(B * i, B * (i + 1))), x3[0:2].reshape(N, Q))
        c3[i, r] = -w
    run(net.gather_x(c3), out, behind=[moves])
    run(moves)
    stores.append(local(c3, col_3))
    for copy in stores:
        copy.wait()
    net.drain()


def product_kernel(sy_ref, w_ref, c3_ref, m_ref, sy, w, c3, wide_w, acc, fwd, end, dma_sems, send_sems, recv_sems):
    net = Net(send_sems, recv_sems)
    z = net.z
    load_3, *loads = [pltpu.make_async_copy(a, b, dma_sems.at[k])
                      for k, (a, b) in enumerate(((c3_ref, c3), (w_ref, w), (sy_ref, sy)))]
    for load in (load_3, *loads):
        load.start()
    net.barrier(*net.zy[2:], net.far_z, net.partner)
    load_3.wait()
    half = pl.ds(2 * net.core, 2)
    parts = []
    for v in range(2):
        wide_w[v, z] = c3[2 * v + z // 2, pl.ds(U * lax.rem(z, 2), U)]
        parts.append((lambda k, v=v: c3.at[2 * v + k // 2, pl.ds(U * lax.rem(k, 2) + 2 * net.core, 2)],
                      lambda k, v=v: wide_w.at[v, k, half]))
    out = net.spread_z(*parts)
    step(out)
    m_ref[...] = jnp.zeros_like(m_ref)

    def block(v, col):
        if v >= 2 and col < 2:
            some = [wide_w[v - 2, k, :, :, B * col:B * (col + 1)] for k in GROUPS]
        else:
            some = [w[v if v == col else U + v // 2, k] for k in GROUPS]
        return jnp.concatenate([x.reshape(H, B) for x in some], axis=1)

    def terms(u, col, groups, more=False):
        part = sum(mm(sy[K * v + Q * u:K * v + Q * (u + 1), :], block(v, col)) for v in groups)
        for k in GROUPS:
            place = k, slice(Q * u, Q * (u + 1)), slice(B * col, B * (col + 1))
            val = part[:, B * k:B * (k + 1)]
            acc[place] = acc[place] + val if more else val

    def sum_of(u):
        def put(k, val):
            m_ref[Q * u + B * k:Q * u + B * (k + 1), :B * (u + 1)] = val

        return net.reduce(acc, fwd, end, Q * u, Q, put, width=B * (u + 1))

    for load in loads:
        load.wait()
    for u in GROUPS:
        for col in range(u + 1):
            terms(u, col, range(col, U if col >= 2 else 2))
        if u == 2:
            step(out)
    run(out)
    sums = []
    for u in GROUPS[::-1]:
        for col in range(min(u + 1, 2)):
            terms(u, col, range(2, U), True)
        for s in sums:
            step(s)
        sums.append(sum_of(u))
        step(sums[-1])
    run(*sums)
    net.drain()


def gradient_kernel(x_ref, own_ref, re_ref, rd_ref, ro_ref, t_ref,
                    wr, terms, acc, fwd, end, dma_sems, send_sems, recv_sems):
    net = Net(send_sems, recv_sems)
    r, c = net.r, net.c
    loads = [[(re_ref.at[0:2, B * u:B * (u + 1)], wr.at[0:2, OFF[u]:OFF[u] + B]),
              (rd_ref.at[:, B * u:B * (u + 1)], wr.at[:, OFF[u] + B:OFF[u] + Q])] for u in GROUPS]
    loads[2] += [(ro_ref.at[:, Q:], wr.at[:, OFF[2] + Q:OFF[3]])]
    loads[0] += [(ro_ref.at[:, :Q], wr.at[:, Q:H])]
    sems = iter(range(16))
    loads = [[pltpu.make_async_copy(a, b, dma_sems.at[next(sems)]) for a, b in some] for some in loads]
    for some in loads[::-1]:
        for load in some:
            load.start()
    net.barrier(net.right, net.left, net.partner, *net.zy)
    for i in GROUPS:
        for k, top in enumerate((H, OFF[1] + Q)):
            wr[net.z, top + B * i:top + B * (i + 1), at(B * net.y)] = own_ref[i, :, B * k:B * (k + 1)]
    rows_0, rows_1 = net.gather_zy(wr, H, H), net.gather_zy(wr, OFF[1] + Q, H)
    step(rows_1)
    step(rows_0)
    t_ref[...] = jnp.zeros_like(t_ref)

    def half_of(u, h):
        width = B * (u + 1)

        def two(x, _):
            a = wr[2 * h + x // 2, group(u), at(Q * lax.rem(x, 2), Q)]
            part = mm_t(a, x_ref[Q * u:, :width])
            for e in range(2):
                terms[x, e, Q * u + B * h:Q * u + B * (h + 1), :width] = part[B * e:B * (e + 1)]
            return 0

        lax.fori_loop(0, U, two, 0)

    def sum_of(u):
        wr[2:, OFF[u]:OFF[u] + B] = jnp.zeros((2, B, H), jnp.float32)
        for load in loads[u]:
            load.wait()
        half_of(u, 0)
        yield
        half_of(u, 1)

        def put(k, val):
            t = 2 * u + k
            for v in range(u + 1):
                t_ref[B * t:B * (t + 1), B * v:B * (v + 1)] = phi(val[:, B * v:B * (v + 1)], R * t + r - 2 * R * v - c)

        yield
        yield from net.reduce(acc, fwd, end, Q * u, Q, put, terms, B * (u + 1))

    s0, s1, s2, s3 = [sum_of(u) for u in GROUPS]
    run(chain(s3, s3, s3, rows_1, s2, s3, rows_1, s2, rows_1, s3, s2, rows_1, s2, s3, rows_0, s1, s2, s1, s1, rows_0, s1, s2,
              rows_0, s1, rows_0, s0, s1, s0, s0, s0, s0))
    run(s2, s1, s0)
    net.drain()


def call(kernel, ident, flops, args, in_specs, outs, out_specs, scratch, sems):
    return pl.pallas_call(
        kernel,
        out_shape=[jax.ShapeDtypeStruct(s, jnp.float32) for s in outs],
        in_specs=in_specs,
        out_specs=out_specs,
        scratch_shapes=[*(pltpu.VMEM(s, jnp.float32) for s in scratch), *(pltpu.SemaphoreType.DMA(s) for s in sems)],
        compiler_params=pltpu.CompilerParams(collective_id=ident, has_side_effects=True, vmem_limit_bytes=67 * 10 ** 6),
        cost_estimate=pl.CostEstimate(flops=flops, bytes_accessed=K, transcendentals=0),
    )(*args)


def solution(mesh):
    def local_pass(fac, bar):
        panel, rows, column = (U, ROWS, H), (U, H, H), (U, R, B, B)
        wide_col, cut = (U, R, B, Q), (2, R, ROWS // (2 * R), B)
        lr, wc, s_own = call(
            front_kernel, 0, 1, (fac, bar), [VM] * 2, (panel, column, (2, ROWS // 2, B)), [HB, VM, VM],
            (panel, (R, B, K), (R, B, K), (U, Q, Q), (U, 2, ROWS, B), (U, ROWS, B), (2, ROWS // 2, B), (U, ROWS // 2, B)),
            ((U,), (128,), (128,)))
        sy, w, row_e, row_d, row_o, col_3 = call(
            levels_kernel, 1, 1, (lr, bar, wc, s_own.reshape(cut)), [HB, HB, VM, HB],
            ((U * K, H), (6, U, U, B, B), rows, rows, rows, wide_col), [HB] * 6,
            ((U, K, B), cut, cut, cut, cut, (2, H, H), rows, (U, K, H), rows, (K, B), (U, 2 * R, B, B), rows, rows, column, rows,
             wide_col, column, column, wide_col, (U, 2, Q, B), (U, Q, B), (2, B, B), (U, B, B)),
            ((48,), (192,), (192,)))
        own = lax.dynamic_index_in_dim(col_3, lax.axis_index('row'), 1, keepdims=False)
        m, = call(
            product_kernel, 2, 1, (sy, w, col_3), [HB] * 3, ((K, H),), [VM],
            ((U * K, H), (6, U, U, B, B), wide_col, (2, U, U, B, Q), (U, K, H), (2, H, H), (U, H, H)), ((4,), (48,), (48,)))
        out, = call(
            gradient_kernel, 3, 1, (m, own, row_e, row_d, row_o), [VM] * 2 + [HB] * 3, ((K, H),), [VM],
            (panel, (U, 2, K, H), (U, K, H), (2, H, H), (U, H, H)), ((16,), (64,), (64,)))
        return out

    spec = P(('batch', 'row'), 'col')
    return jax.shard_map(local_pass, mesh=mesh, in_specs=(spec, spec), out_specs=spec, check_vma=False)
```

time: 20000 us -> 582 us (0.03)
  waiting for transfers between devices: 18300 us -> 0 us
  other arithmetic: 1000 us -> 0 us
  matrix products: 619 us -> 0 us
  Pallas kernels: 0 us -> 567 us
    psum x256 -> x0, waiting for transfers between devices: 18300 us -> none  [the longest x64 5340 us: block_step(): c_bar_all = lax.psum(jnp.where(keep_solved, solved, 0.0), 'col')]
    another operation x128 -> x0, other arithmetic: 682 us -> none  [block_step(): lax.linalg.triangular_solve(d_fac, t_panel, left_side=False, lower=True)]
    pallas_call x0 -> x4, Pallas kernels: none -> 567 us  [call(): pl.pallas_call(kernel, out_shape=[jax.ShapeDtypeStruct(s, jnp.float32) fo...]
    dot_general x256 -> x0, matrix products: 551 us -> none  [the longest x64 249 us: block_step(): jnp.einsum('ri,rc->ic', c_bar_all, chol_loc, precision=PREC_HIGH, preferr...]
    select_n x256 -> x0, other arithmetic: 311 us -> none  [the longest x64 108 us: block_step(): r_fac = lax.psum(jnp.where(on_row & left_mask, l_row, 0.0), 'row')]
  transfers between devices with their start and end apart: 256 -> 0, of which waited for: 256 -> 0; matrix products, arithmetic and copies ran while one was open for 1% -> 0% of each run, Pallas kernels for 0% -> 0%
where the time goes in v1:
time: 582 us; the launch traced here: 573 us
  Pallas kernels  567 us (97%)
    pallas_call x4, Pallas kernels, call(): pl.pallas_call(kernel, out_shape=[jax.ShapeDtypeStruct(s, jnp.float32) fo...  567 us

profile of v1, /device:TPU:1, one launch (start us, length us, event | category | flops | bytes accessed | tf_op | source)
XLA Modules:
  0.0 572.8 jit_solution(3635959089394171474)
XLA Ops:
  0.0 152.0 %shard_map.28 = (f32[4,2560,512]{2,1,0:T(8,128)}, f32[4,8,128,128]{3,2,1,0:T(8,128)}, f32[2,1280,128]{2,1,0:T(8,128)}) custom-call(f32[1024,512]{1,0:T(8,128)} %l_ref.1, f32[1024,512]{1,0:T(8,128)} %bar_ref.3), custom_call_target="tpu_custom_call" | custom-call | flops 1 | bytes 1024 | tf_op jit(solution)/shard_map/pallas_call | solution.py:667
  152.1 247.4 %shard_map.29 = (f32[4096,512]{1,0:T(8,128)}, f32[6,4,4,128,128]{4,3,2,1,0:T(8,128)}, f32[4,512,512]{2,1,0:T(8,128)}, f32[4,512,512]{2,1,0:T(8,128)}, f32[4,512,...) custom-call(f32[4,2560,512]{2,1,0:T(8,128)} %get-tuple-element.14.lr_ref, f32[1024,512]{1,0:T(8,128)} %bar_ref.3, ...), custom_call_target="tpu_custom_call" | custom-call | flops 1 | bytes 1024 | tf_op jit(solution)/shard_map/pallas_call | solution.py:667
  399.4 82.0 %shard_map.30.x_ref = f32[1024,512]{1,0:T(8,128)} custom-call(f32[4096,512]{1,0:T(8,128)} %get-tuple-element.17.sy_ref, f32[6,4,4,128,128]{4,3,2,1,0:T(8,128)} %get-tuple-element.18.w_ref, f32[4,8,128,256]{3,2,1,0:T(8,128)} %get-tuple-element.19.c3_ref), custom_call_target="tpu_custom_call" | custom-call | flops 1 | bytes 1024 | tf_op jit(solution)/shard_map/pallas_call | solution.py:667
  481.5 1.9 dynamic-slice_bitcast_fusion.own_ref
  483.3 86.0 %shard_map.31 = f32[1024,512]{1,0:T(8,128)} custom-call(f32[1024,512]{1,0:T(8,128)} %shard_map.30.x_ref, f32[4,128,256]{2,1,0:T(8,128)} %dynamic-slice_bitcast_fusion.own_ref, f32[4,512,512]{2,1,0:T(8,128)} %get-tuple-element.20.re_ref, f32[4,512,512]{2,1,0:T(8,128)} %get-tuple-element.21.rd_ref, f32[4,512,512]{2,1,0:T(8,128)} %get-tuple-element.22.ro_ref), custom_call_target="tpu_custom_call" | custom-call | flops 1 | bytes 1024 | tf_op jit(solution)/shard_map/pallas_call | solution.py:667
  569.3 3.1 copy.4

commit v2 on v1

--- a/solution.py
+++ b/solution.py
@@ -116,16 +116,21 @@
             return ref.at[(other, first + r) if axis else (r, other)]
 
         near_r, near_l, far = [2 * mod4(self.x + d) + self.core for d in (1, -1, 2)]
-        to_right, to_left = self.copy(view(self.r), self.right), self.copy(view(self.r), self.left)
+        to_right, to_left = [], []
+        for part in range(2):
+            to_right.append(self.copy(view(self.r, part), self.right))
+            to_left.append(self.copy(view(self.r, 1 - part), self.left))
         over = [self.copy(view(self.r), self.partner)]
         yield
-        to_right.wait_recv()
+        to_right[0].wait_recv()
         far_0 = self.copy(view(near_l, 0), self.right)
+        to_left[0].wait_recv()
+        far_1 = self.copy(view(near_r, 1), self.left)
+        yield
+        to_right[1].wait_recv()
         over.append(self.copy(view(near_l), self.partner))
-        to_left.wait_recv()
-        far_1 = self.copy(view(near_r, 1), self.left)
+        to_left[1].wait_recv()
         over.append(self.copy(view(near_r), self.partner))
-        yield
         far_0.wait_recv()
         over.append(self.copy(view(far, 0), self.partner))
         far_1.wait_recv()
@@ -135,43 +140,53 @@
             copy.wait_recv()
         yield
 
-    def gather_zy(self, ref, start, count):
+    def gather_zy(self, ref, start, count, first, thin=0):
         yp, ym, zp, zm = self.zy
-        y, z, n = self.y, self.z, count // U
+        y, z = self.y, self.z
         y_m, y_p, z_m, z_p = mod4(y - 1), mod4(y + 1), mod4(z - 1), mod4(z + 1)
 
-        def view(zs, part, ys=None, parts=1):
-            return ref.at[zs, pl.ds(start + part * n, parts * n), ALL if ys is None else at(B * ys)]
-
-        def both(first, second, to_first, to_second):
-            return self.copy(first, to_first), self.copy(second, to_second)
-
-        a = both(view(z, 0, y, 2), view(z, 0, y, 2), yp, ym)
-        b = both(view(z, 2, y, 2), view(z, 2, y, 2), zp, zm)
-        yield
-        for copy in a:
-            copy.wait_recv()
-        a = both(view(z, 0, y_m), view(z, 1, y_p), yp, ym)
-        for copy in b:
-            copy.wait_recv()
-        b = both(view(z_m, 2, y), view(z_p, 3, y), zp, zm)
-        yield
-        for copy in a:
-            copy.wait_recv()
-        a = both(view(z, 0, None, 2), view(z, 0, None, 2), zp, zm)
-        for copy in b:
-            copy.wait_recv()
-        b = both(view(ALL, 2, y, 2), view(ALL, 2, y, 2), yp, ym)
-        yield
-        for copy in a:
-            copy.wait_recv()
-        a = both(view(z_m, 0), view(z_p, 1), zp, zm)
-        for copy in b:
-            copy.wait_recv()
-        b = both(view(ALL, 2, y_m), view(ALL, 3, y_p), yp, ym)
-        yield
-        for copy in (*a, *b):
-            copy.wait_recv()
+        def cut(top, size):
+            return pl.ds(top, size // 2), pl.ds(top + size // 2, size // 2), pl.ds(top, size)
+
+        a_0, a_1, a_all = cut(start + count - first, first)
+        b_0, b_1, b_all = cut(start, count - first)
+        c_0, c_1, c_all = cut(start + thin, count - first - thin)
+        t_0, t_1, t_all = cut(start, thin)
+        front = slice(0, 2)
+
+        def both(zs, rows, to, ys=None, zs_back=None, rows_back=None, ys_back=None):
+            lane, lane_back = [ALL if v is None else at(B * v) for v in (ys, ys_back)]
+            forth = ref.at[zs, rows, lane]
+            back = forth if rows_back is None else ref.at[zs_back, rows_back, lane_back]
+            return self.copy(forth, to[0]), self.copy(back, to[1])
+
+        def done(*copies):
+            for copy in copies:
+                copy.wait_recv()
+
+        on_y, on_z = (yp, ym), (zp, zm)
+        a, b = both(z, a_all, on_y, y), both(z, b_all, on_z, y)
+        yield
+        done(*a)
+        a = both(z, a_0, on_y, y_m, z, a_1, y_p)
+        done(*b)
+        b = both(z_m, b_0, on_z, y, z_p, b_1, y)
+        yield
+        done(*a)
+        a = both(z, a_all, on_z)
+        done(*b)
+        b = both(ALL, c_all, on_y, y)
+        if thin:
+            b += both(front, t_all, on_y, y)
+        yield
+        done(*a)
+        a = both(z_m, a_0, on_z, None, z_p, a_1)
+        done(*b)
+        b = both(ALL, c_0, on_y, y_m, ALL, c_1, y_p)
+        if thin:
+            b += both(front, t_0, on_y, y_m, front, t_1, y_p)
+        yield
+        done(*a, *b)
         yield
 
     def gather_y(self, ref, start, count):
@@ -207,20 +222,16 @@
             copy.wait_recv()
         yield
 
-    def transpose(self, a, b, d, out):
-        def on_line(k):
-            return ALL, k
-
-        def on_plane(k):
-            return k // R, lax.rem(k, R)
-
-        line, plane = (self.line(), self.r, on_line), (self.plane(), self.c, on_plane)
-        for src, dst, (others, me, piece) in ((a, b, line), (b, d, plane), (d, out, line)):
-            sent = [self.copy(src.at[piece(place)], peer, dst.at[piece(me)]) for peer, place in others]
-            dst[piece(me)] = src[piece(me)]
-            yield
-            for copy in sent:
-                copy.wait_recv()
+    def swap(self, src, dst, across):
+        def piece(k):
+            return (k // R, lax.rem(k, R)) if across else (ALL, k)
+
+        others, me = (self.plane(), self.c) if across else (self.line(), self.r)
+        sent = [self.copy(src.at[piece(place)], peer, dst.at[piece(me)]) for peer, place in others]
+        dst[piece(me)] = src[piece(me)]
+        yield
+        for copy in sent:
+            copy.wait_recv()
         yield
 
     def reduce(self, acc, fwd, end, start, count, put, terms=None, width=None):
@@ -302,26 +313,37 @@
         size *= 2
 
 
+def pieces(ref, u, v):
+    top, n = B * (u * (u + 1) // 2 + v - 1), ref.shape[2]
+    i, low = top // n, top % n
+    cut = min(B, n - low)
+    first = [(slice(0, cut), (i, slice(low, low + cut)))]
+    return first if cut == B else first + [(slice(cut, B), (i + 1, slice(0, B - cut)))]
+
+
 def inner(net, u, start, panel, top, bar, terms):
     def two(k, _):
         h, x = k // U, lax.rem(k, U)
-        p = mm_t(panel[2 * h + x // 2, top:top + K - Q * u, at(Q * lax.rem(x, 2), Q)], bar[Q * u:, :B * (u + 1)])
+        a, b = panel[2 * h + x // 2, top:top + K - Q * u, at(Q * lax.rem(x, 2), Q)], bar[Q * u:, :B * (u + 1)]
+        p = mm_t(a, b) if u else mm_t(b, a)
         for e in range(2):
             for v in range(u + 1):
-                val = p[B * e:B * (e + 1), B * v:B * (v + 1)]
+                val = p[B * e:B * (e + 1), B * v:B * (v + 1)] if u else p[:, B * e:B * (e + 1)].T
                 terms[x, e, at(start + Q * v + B * h), :] = phi(val, 2 * k + e - net.c) if v == u else val
         return 0
 
     lax.fori_loop(0, R, two, 0)
 
 
-def front_kernel(l_ref, bar_ref, lr_ref, col_ref, s_ref, lv, lss, wss, tmp, terms, acc, fwd, end, dma_sems, send_sems, recv_sems):
+def front_kernel(l_ref, bar_ref, lr_ref, col_ref, a_ref, b_ref, lv, lss, wss, tmp, terms, acc, fwd, end, dma_sems, send_sems, recv_sems):
     net = Net(send_sems, recv_sems)
     r, c, y, z, core = net.r, net.c, net.y, net.z, net.core
     half, zz = z // 2, lax.rem(z, 2)
     ways = (1, 2, 3)
     others = [net.device(y=mod4(y + d)) for d in ways]
-    net.barrier(net.right, net.left, net.partner, *others, *net.zy[2:])
+    for u in GROUPS:
+        lv[2:, OFF[u]:OFF[u] + B] = jnp.zeros((2, B, H), jnp.float32)
+    net.barrier(*[peer for peer, _ in net.line()], *others, *net.zy[2:])
 
     strip = at(B * (U * zz + y))
 
@@ -332,7 +354,7 @@
     lss[r, :, strip] = l_ref[own(y)]
     for u in GROUPS:
         lv[z, group(u), at(B * y)] = l_ref[Q * u:, B * u:B * (u + 1)]
-    g = [net.gather_zy(lv, OFF[u], K - Q * u) for u in GROUPS]
+    g = [net.gather_zy(lv, OFF[u], K - Q * u, (K - Q * u - 96) // 2, B) for u in GROUPS]
     run(chain(g[3], g[2]))
     for copy in sent:
         copy.wait_recv()
@@ -358,7 +380,8 @@
 
         def put(k, val):
             v, h = k // 2, k % 2
-            s_ref[h, B * (u * (u + 1) // 2 + v):B * (u * (u + 1) // 2 + v + 1), :] = val
+            for rows, place in pieces(a_ref, u, v):
+                a_ref[(h, *place)] = val[rows]
 
         keep(u)
         return net.reduce(acc, fwd, end, start, Q * (u + 1), put, terms)
@@ -383,31 +406,31 @@
     step(s2)
     tick()
 
-    mine = pl.ds(U * core, U)
-    sent = [net.copy(wss.at[mine, :, at(B * (U * zz + mod4(y + d)))], other, col_ref.at[y, mine]) for d, other in zip(ways, others)]
-    col_ref[y] = wss[:, :, strip]
+    sent = [net.copy(wss.at[r, :, at(B * (U * zz + mod4(y + d)))], other, col_ref.at[y, r]) for d, other in zip(ways, others)]
+    col_ref[y, r] = wss[r, :, strip]
     step(s2)
     tick()
     tick()
     s1 = begin(1)
     run(s3, s2)
-    over = []
-    for d, copy in zip(ways, sent):
+    for copy in sent:
         copy.wait_recv()
-        over.append(net.copy(col_ref.at[mod4(y - d), mine], net.partner))
-    run(s1)
+    columns = net.gather_x(col_ref)
+    step(columns)
+    run(s1, columns)
+    flip = net.swap(a_ref, b_ref, False)
+    step(flip)
     for _ in range(U):
         tick()
+    step(flip)
     keep(0)
-    for copy in over:
-        copy.wait_recv()
     for copy in stores:
         copy.wait()
     net.drain()
 
 
-def levels_kernel(lr_ref, bar_ref, wc_ref, s_ref, sy_ref, w_ref, row_e, row_d, row_o, col_3,
-                  own, a, b, d, back, la, lb, l0, l1, bv, cd, re, rd, co, ro, c3, x1, x2, x3, terms, acc, fwd, end, dma_sems, send_sems, recv_sems):
+def levels_kernel(lr_ref, bar_ref, wc_ref, a, b, sy_ref, w_ref, row_e, row_d, row_o, col_3,
+                  own, d, back, s_top, top_back, la, lb, l0, l1, bv, cd, re, rd, co, ro, c3, x1, x2, x3, terms, acc, fwd, end, dma_sems, send_sems, recv_sems, t_send, t_recv):
     net = Net(send_sems, recv_sems)
     r, c, y, z = net.r, net.c, net.y, net.z
     sems = iter(range(32))
@@ -417,27 +440,28 @@
         copy.start()
         return copy
 
-    load_s = local(s_ref, a)
     load_0 = [local(lr_ref.at[:, group(0)], l0), local(bar_ref.at[:, 0:B], bv)]
     load_a = [local(lr_ref.at[0:2, OFF[u] + B:OFF[u] + Q], la.at[:, B * u:B * (u + 1)]) for u in GROUPS]
     load_b = [local(lr_ref.at[:, OFF[u] + Q:OFF[u] + H], lb.at[:, B * u:B * (u + 2)]) for u in (0, 2)]
     load_c = local(lr_ref.at[:, OFF[1] + Q:OFF[2]], l1)
     net.barrier(*[peer for peer, _ in net.line() + net.plane()])
-    piece = a.shape[2]
-
-    def block(ref, k, u, v):
-        top = B * (u * (u + 1) // 2 + v)
-        i, low = top // piece, top % piece
-        first = ref[k, i, low:low + B]
-        return first if low + B <= piece else jnp.concatenate([first, ref[k, i + 1, :low + B - piece]], axis=0)
+    half_c, row_c = c // R, lax.rem(c, R)
+    swap = [{'row': row_c, 'col': r + R * h} for h in range(2)]
+    away = [(row_c != r) | (half_c != h) for h in range(2)]
+
+    def block(ref, h, u, v):
+        return jnp.concatenate([ref[(h, *place)] for _, place in pieces(ref, u, v)], axis=0)
+
+    def trade(h, slot):
+        return pltpu.make_async_remote_copy(src_ref=s_top.at[h], dst_ref=top_back.at[slot], send_sem=t_send.at[h],
+                                            recv_sem=t_recv.at[slot], device_id=swap[h], device_id_type=MESH)
 
     low = c < R
     stores = []
     for u in GROUPS:
         re[z, B * u:B * (u + 1), at(B * y)] = wc_ref[u, r]
-    diag = net.gather_zy(re, 0, H)
+    diag = net.gather_zy(re, 0, H, Q)
     step(diag)
-    load_s.wait()
     for u in range(1, U):
         for h in range(2):
             for v in range(u + 1):
@@ -446,47 +470,55 @@
     for place in places:
         place.wait()
     early = [net.gather_y(sy_ref, K * v + Q * (v + 1), K - Q * (v + 1)) for v in range(U - 1)]
-    late = [net.gather_y(sy_ref, K * v, Q * (v + 1)) for v in GROUPS]
-    moves = chain(*[early[k] for k in (0, 1, 0, 2, 1, 0, 2, 1, 2)])
+    late = net.gather_y(sy_ref, 3 * K, K)
+    e0, e1, e2 = early
     half = pl.ds(2 * net.core, 2)
-    step(moves)
+    step(e0)
 
     for u in GROUPS:
         load_a[u].wait()
         cd[u, 0:R] = jnp.where(low, wc_ref[u], 0.0)
         x1[u, r] = mm(wide(la, slice(B * u, B * (u + 1)), (0, 1)), cd[u, 0:R].reshape(K, B))
     strips = net.gather_x(x1)
-    step(strips)
+    flip = net.swap(b, d, True)
+    run(chain(strips, diag, strips, diag, flip))
     for load in load_0:
         load.wait()
     inner(net, 0, 0, l0, 0, bv, terms)
 
     def put(k, val):
-        a[k, 0, :B] = val
-
-    run(strips, net.reduce(acc, fwd, end, 0, Q, put, terms), diag)
-    flip = net.transpose(a, b, d, back)
-    step(flip)
+        s_top[k] = val
+
+    run(strips, net.reduce(acc, fwd, end, 0, Q, put, terms), behind=[chain(diag, e0, diag)])
+    run(diag)
+    for h in range(2):
+        @pl.when(away[h])
+        def _():
+            trade(h, half_c).start()
+
+        @pl.when(jnp.logical_not(away[h]))
+        def _():
+            top_back[h] = s_top[h]
     stores.append(local(re, row_e))
     for u in GROUPS:
         w = -mm(wide(re, slice(B * u, B * (u + 1)), (2, 3)), x1[u].reshape(K, B))
         w = jnp.where(low, w, wc_ref[u, r])
         cd[u, R + r] = w
         rd[z, B * u:B * (u + 1), at(B * y)] = w
-    rows = net.gather_zy(rd, 0, H)
+    rows = net.gather_zy(rd, 0, H, Q)
     step(rows)
-    run(net.gather_x(cd, first=R), behind=[rows, moves])
+    run(net.gather_x(cd, first=R), behind=[chain(rows, e1, rows, e0)])
     stores.append(local(cd.at[:, pl.ds(U * z, U)], w_ref.at[0:U, z]))
     out = net.spread_z((lambda k: cd.at[:, pl.ds(U * k + 2 * net.core, 2)], lambda k: w_ref.at[0:U, k, half]))
-    step(out)
-    moves = chain(moves, moves, moves, out, out)
+    step(flip)
+    flip = net.swap(d, back, False)
     step(flip)
 
     for q in range(2):
         load_b[q].wait()
         x2[2 * q:2 * q + 2, r] = mm(wide(lb, slice(Q * q, Q * (q + 1))), cd[2 * q].reshape(N, B)).reshape(2, B, B)
-    run(net.gather_x(x2), rows, behind=[moves])
-    step(flip)
+    run(net.gather_x(x2), behind=[chain(e1, rows, e2, e1)])
+    run(rows)
     stores.append(local(rd, row_d))
     for q in range(2):
         at_u = slice(B * (2 * q + 1), B * (2 * q + 2))
@@ -494,40 +526,42 @@
         for i, w in enumerate(tops):
             co[2 * q + i, r] = -w
             ro[z, B * (2 * q + i):B * (2 * q + i + 1), at(B * y)] = -w
-    rows = net.gather_zy(ro, 0, H)
+    rows = net.gather_zy(ro, 0, H, Q)
     step(rows)
-    run(net.gather_x(co), behind=[rows, moves])
-    run(moves)
+    step(out)
+    strips = net.gather_x(co)
+    step(strips)
+
+    step(flip)
+    for h in range(2):
+        own[0, B * h:B * (h + 1), :] = s_top[h]
+    for s in range(2):
+        @pl.when(away[s])
+        def _():
+            trade(s, s).wait_recv()
+        for u in GROUPS:
+            for v in range(u + 1):
+                at_t = slice(B * (2 * v + s), B * (2 * v + s + 1))
+                val = (block(back, s, u, v) if u else top_back[s]).T
+                own[u, at_t, :] = own[u, at_t, :] + val if u == v else val
+    places = [local(own.at[v, 0:Q * (v + 1)], sy_ref.at[K * v:K * v + Q * (v + 1), at(B * y)]) for v in GROUPS]
+    run(strips, behind=[chain(rows, e2, rows, out)])
+    for place in places:
+        place.wait()
+    step(late)
     parts = []
     for q in range(2):
         stores.append(local(co.at[2 * q + z // 2, pl.ds(U * lax.rem(z, 2), U)], w_ref.at[U + q, z]))
         parts.append((lambda k, q=q: co.at[2 * q + k // 2, pl.ds(U * lax.rem(k, 2) + 2 * net.core, 2)],
                       lambda k, q=q: w_ref.at[U + q, k, half]))
-    out = net.spread_z(*parts)
-    step(out)
+    out_o = net.spread_z(*parts)
 
     load_c.wait()
     x3[:, r] = mm(wide(l1, ALL), jnp.concatenate([co[0:2].reshape(N, B), cd[1].reshape(N, B)], 1)).reshape(U, B, Q)
     x3[:, r, :, :B] = x3[:, r, :, :B] + mm(wide(l0, slice(H, K)), cd[0].reshape(N, B)).reshape(U, B, B)
-    strips = net.gather_x(x3)
-    step(strips)
-
-    step(flip)
-    for h in range(2):
-        own[0, B * h:B * (h + 1), :] = block(a, h, 0, 0)
-    for s in range(2):
-        for u in GROUPS:
-            for v in range(u + 1):
-                at_t = slice(B * (2 * v + s), B * (2 * v + s + 1))
-                val = block(back, s, u, v).T
-                own[u, at_t, :] = own[u, at_t, :] + val if u == v else val
-    places = [local(own.at[v, 0:Q * (v + 1)], sy_ref.at[K * v:K * v + Q * (v + 1), at(B * y)]) for v in GROUPS]
-    run(strips, rows)
-    for place in places:
-        place.wait()
-    moves = chain(*[late[k] for k in (3, 2, 3, 1, 2, 3, 0, 1, 2, 0, 1, 0)])
-    step(moves)
-    step(moves)
+    run(net.gather_x(x3), behind=[chain(rows, late, out, e2)])
+    run(rows)
+    step(out_o)
     stores.append(local(ro, row_o))
     for i in GROUPS:
         u = 2 + i // 2
@@ -539,23 +573,30 @@
         if i >= 2:
             w = w + mm(wide(ro, slice(B * i, B * (i + 1))), x3[0:2].reshape(N, Q))
         c3[i, r] = -w
-    run(net.gather_x(c3), out, behind=[moves])
-    run(moves)
+    run(net.gather_x(c3), behind=[chain(late, out_o)])
+    run(late, out_o)
     stores.append(local(c3, col_3))
+    for h in range(2):
+        @pl.when(away[h])
+        def _():
+            trade(h, half_c).wait_send()
     for copy in stores:
         copy.wait()
     net.drain()
 
 
-def product_kernel(sy_ref, w_ref, c3_ref, m_ref, sy, w, c3, wide_w, acc, fwd, end, dma_sems, send_sems, recv_sems):
+def product_kernel(sy_ref, w_ref, c3_ref, m_ref, own_ref, sy, w, c3, wide_w, acc, fwd, end, dma_sems, send_sems, recv_sems):
     net = Net(send_sems, recv_sems)
     z = net.z
-    load_3, *loads = [pltpu.make_async_copy(a, b, dma_sems.at[k])
-                      for k, (a, b) in enumerate(((c3_ref, c3), (w_ref, w), (sy_ref, sy)))]
-    for load in (load_3, *loads):
+    start = [slice(K * v, K * v + Q * (v + 1)) for v in range(U - 1)]
+    rest = [slice(K * v + Q * (v + 1), K * (v + 1)) for v in range(U - 1)] + [slice(3 * K, U * K)]
+    loads = [(c3_ref, c3), *[(sy_ref.at[some], sy.at[some]) for some in (*start, *rest)], (w_ref, w)]
+    loads = [pltpu.make_async_copy(a, b, dma_sems.at[k]) for k, (a, b) in enumerate(loads)]
+    for load in loads:
         load.start()
-    net.barrier(*net.zy[2:], net.far_z, net.partner)
-    load_3.wait()
+    for load in loads[:U]:
+        load.wait()
+    net.barrier(*net.zy, net.far_z, net.partner)
     half = pl.ds(2 * net.core, 2)
     parts = []
     for v in range(2):
@@ -564,6 +605,9 @@
                       lambda k, v=v: wide_w.at[v, k, half]))
     out = net.spread_z(*parts)
     step(out)
+    own_ref[...] = c3[:, net.r]
+    m0, m1, m2 = moves = [net.gather_y(sy, K * v, Q * (v + 1)) for v in range(U - 1)]
+    run(chain(m2, m1))
     m_ref[...] = jnp.zeros_like(m_ref)
 
     def block(v, col):
@@ -586,30 +630,29 @@
 
         return net.reduce(acc, fwd, end, Q * u, Q, put, width=B * (u + 1))
 
-    for load in loads:
+    for load in loads[U:]:
         load.wait()
-    for u in GROUPS:
+    sums = []
+    for u in GROUPS[::-1]:
         for col in range(u + 1):
             terms(u, col, range(col, U if col >= 2 else 2))
-        if u == 2:
-            step(out)
-    run(out)
-    sums = []
-    for u in GROUPS[::-1]:
+        if u == 3:
+            run(chain(m2, m0, m1, m2, out))
+            run(out)
         for col in range(min(u + 1, 2)):
             terms(u, col, range(2, U), True)
         for s in sums:
             step(s)
         sums.append(sum_of(u))
         step(sums[-1])
-    run(*sums)
+        run(chain(m1, m0))
+    run(*moves, *sums)
     net.drain()
 
 
 def gradient_kernel(x_ref, own_ref, re_ref, rd_ref, ro_ref, t_ref,
                     wr, terms, acc, fwd, end, dma_sems, send_sems, recv_sems):
     net = Net(send_sems, recv_sems)
-    r, c = net.r, net.c
     loads = [[(re_ref.at[0:2, B * u:B * (u + 1)], wr.at[0:2, OFF[u]:OFF[u] + B]),
               (rd_ref.at[:, B * u:B * (u + 1)], wr.at[:, OFF[u] + B:OFF[u] + Q])] for u in GROUPS]
     loads[2] += [(ro_ref.at[:, Q:], wr.at[:, OFF[2] + Q:OFF[3]])]
@@ -623,19 +666,22 @@
     for i in GROUPS:
         for k, top in enumerate((H, OFF[1] + Q)):
             wr[net.z, top + B * i:top + B * (i + 1), at(B * net.y)] = own_ref[i, :, B * k:B * (k + 1)]
-    rows_0, rows_1 = net.gather_zy(wr, H, H), net.gather_zy(wr, OFF[1] + Q, H)
+    rows_0, rows_1 = net.gather_zy(wr, H, H, Q), net.gather_zy(wr, OFF[1] + Q, H, Q)
     step(rows_1)
     step(rows_0)
-    t_ref[...] = jnp.zeros_like(t_ref)
-
-    def half_of(u, h):
+
+    def half_of(u, h, top=0, rows=K):
         width = B * (u + 1)
+        some = slice(OFF[u] + top, min(OFF[u] + top + rows, OFF[u] + K - Q * u))
+        these = slice(Q * u + top, Q * u + top + some.stop - some.start)
 
         def two(x, _):
-            a = wr[2 * h + x // 2, group(u), at(Q * lax.rem(x, 2), Q)]
-            part = mm_t(a, x_ref[Q * u:, :width])
+            a, b = wr[2 * h + x // 2, some, at(Q * lax.rem(x, 2), Q)], x_ref[these, :width]
+            part = mm_t(a, b) if u else mm_t(b, a)
             for e in range(2):
-                terms[x, e, Q * u + B * h:Q * u + B * (h + 1), :width] = part[B * e:B * (e + 1)]
+                place = x, e, slice(Q * u + B * h, Q * u + B * (h + 1)), slice(0, width)
+                val = part[B * e:B * (e + 1)] if u else part[:, B * e:B * (e + 1)].T
+                terms[place] = terms[place] + val if top else val
             return 0
 
         lax.fori_loop(0, U, two, 0)
@@ -644,21 +690,19 @@
         wr[2:, OFF[u]:OFF[u] + B] = jnp.zeros((2, B, H), jnp.float32)
         for load in loads[u]:
             load.wait()
-        half_of(u, 0)
-        yield
-        half_of(u, 1)
+        for top in ((0,) if u else (0, H)):
+            for h in range(2):
+                half_of(u, h, top, K if u else H)
+                yield
 
         def put(k, val):
-            t = 2 * u + k
-            for v in range(u + 1):
-                t_ref[B * t:B * (t + 1), B * v:B * (v + 1)] = phi(val[:, B * v:B * (v + 1)], R * t + r - 2 * R * v - c)
-
-        yield
+            t_ref[B * (2 * u + k):B * (2 * u + k + 1), :B * (u + 1)] = val
+
         yield from net.reduce(acc, fwd, end, Q * u, Q, put, terms, B * (u + 1))
 
     s0, s1, s2, s3 = [sum_of(u) for u in GROUPS]
-    run(chain(s3, s3, s3, rows_1, s2, s3, rows_1, s2, rows_1, s3, s2, rows_1, s2, s3, rows_0, s1, s2, s1, s1, rows_0, s1, s2,
-              rows_0, s1, rows_0, s0, s1, s0, s0, s0, s0))
+    run(chain(s3, s3, s3, rows_1, s2, s3, rows_1, s2, rows_1, s3, s2, rows_1, s2, s3, rows_0, s1, s2, s1, s1, rows_0, s0, s1, s2,
+              s0, s1, rows_0, s1, rows_0, s0, s0, s0, s0, s0, s0))
     run(s2, s1, s0)
     net.drain()
 
@@ -678,25 +722,27 @@
 def solution(mesh):
     def local_pass(fac, bar):
         panel, rows, column = (U, ROWS, H), (U, H, H), (U, R, B, B)
-        wide_col, cut = (U, R, B, Q), (2, R, ROWS // (2 * R), B)
-        lr, wc, s_own = call(
-            front_kernel, 0, 1, (fac, bar), [VM] * 2, (panel, column, (2, ROWS // 2, B)), [HB, VM, VM],
+        wide_col, cut = (U, R, B, Q), (2, R, (ROWS - Q) // (2 * R), B)
+        lr, wc, a, b = call(
+            front_kernel, 0, 1, (fac, bar), [VM] * 2, (panel, column, cut, cut), [HB] + [VM] * 3,
             (panel, (R, B, K), (R, B, K), (U, Q, Q), (U, 2, ROWS, B), (U, ROWS, B), (2, ROWS // 2, B), (U, ROWS // 2, B)),
-            ((U,), (128,), (128,)))
+            ((U,), (144,), (144,)))
         sy, w, row_e, row_d, row_o, col_3 = call(
-            levels_kernel, 1, 1, (lr, bar, wc, s_own.reshape(cut)), [HB, HB, VM, HB],
+            levels_kernel, 1, 1, (lr, bar, wc, a, b), [HB, HB, VM, VM, VM],
             ((U * K, H), (6, U, U, B, B), rows, rows, rows, wide_col), [HB] * 6,
-            ((U, K, B), cut, cut, cut, cut, (2, H, H), rows, (U, K, H), rows, (K, B), (U, 2 * R, B, B), rows, rows, column, rows,
+            ((U, K, B), cut, cut, (2, B, B), (2, B, B), (2, H, H), rows, (U, K, H), rows, (K, B), (U, 2 * R, B, B), rows, rows, column, rows,
              wide_col, column, column, wide_col, (U, 2, Q, B), (U, Q, B), (2, B, B), (U, B, B)),
-            ((48,), (192,), (192,)))
-        own = lax.dynamic_index_in_dim(col_3, lax.axis_index('row'), 1, keepdims=False)
-        m, = call(
-            product_kernel, 2, 1, (sy, w, col_3), [HB] * 3, ((K, H),), [VM],
-            ((U * K, H), (6, U, U, B, B), wide_col, (2, U, U, B, Q), (U, K, H), (2, H, H), (U, H, H)), ((4,), (48,), (48,)))
+            ((48,), (208,), (208,), (2,), (2,)))
+        m, own = call(
+            product_kernel, 2, 1, (sy, w, col_3), [HB] * 3, ((K, H), (U, B, Q)), [VM] * 2,
+            ((U * K, H), (6, U, U, B, B), wide_col, (2, U, U, B, Q), (U, K, H), (2, H, H), (U, H, H)), ((16,), (48,), (48,)))
         out, = call(
             gradient_kernel, 3, 1, (m, own, row_e, row_d, row_o), [VM] * 2 + [HB] * 3, ((K, H),), [VM],
             (panel, (U, 2, K, H), (U, K, H), (2, H, H), (U, H, H)), ((16,), (64,), (64,)))
-        return out
+        row, col = lax.broadcasted_iota(jnp.int32, out.shape, 0), lax.broadcasted_iota(jnp.int32, out.shape, 1)
+        row_all = (row // B * R + lax.axis_index('row')) * B + row % B
+        col_all = (col // B * 2 * R + lax.axis_index('col')) * B + col % B
+        return jnp.where(row_all > col_all, out, jnp.where(row_all == col_all, 0.5 * out, 0.0))
 
     spec = P(('batch', 'row'), 'col')
     return jax.shard_map(local_pass, mesh=mesh, in_specs=(spec, spec), out_specs=spec, check_vma=False)

time: 582 us -> 525 us (0.902)
  Pallas kernels: 567 us -> 511 us
    pallas_call x4, Pallas kernels: 567 us -> 511 us  [call(): pl.pallas_call(kernel, out_shape=[jax.ShapeDtypeStruct(s, jnp.float32) fo...]
where the time goes in v2:
time: 525 us; the launch traced here: 515 us
  Pallas kernels  511 us (97%)
    pallas_call x4, Pallas kernels, call(): pl.pallas_call(kernel, out_shape=[jax.ShapeDtypeStruct(s, jnp.float32) fo...  511 us

profile of v2, /device:TPU:1, one launch (start us, length us, event | category | flops | bytes accessed | tf_op | source)
XLA Modules:
  0.0 515.4 jit_solution(11208763597309876652)
XLA Ops:
  0.0 157.1 %shard_map.28 = (f32[4,2560,512]{2,1,0:T(8,128)}, f32[4,8,128,128]{3,2,1,0:T(8,128)}, f32[2,8,144,128]{3,2,1,0:T(8,128)}, f32[2,8,144,128]{3,2,1,0:T(8,128)}) custom-call(f32[1024,512]{1,0:T(8,128)} %l_ref.1, f32[1024,512]{1,0:T(8,128)} %bar_ref.3), custom_call_target="tpu_custom_call" | custom-call | flops 1 | bytes 1024 | tf_op jit(solution)/shard_map/pallas_call | solution.py:711
  157.1 194.3 %shard_map.29 = (f32[4096,512]{1,0:T(8,128)}, f32[6,4,4,128,128]{4,3,2,1,0:T(8,128)}, f32[4,512,512]{2,1,0:T(8,128)}, f32[4,512,512]{2,1,0:T(8,128)}, f32[4,512,...) custom-call(f32[4,2560,512]{2,1,0:T(8,128)} %get-tuple-element.17.lr_ref, f32[1024,512]{1,0:T(8,128)} %bar_ref.3, ...), custom_call_target="tpu_custom_call" | custom-call | flops 1 | bytes 1024 | tf_op jit(solution)/shard_map/pallas_call | solution.py:711
  351.4 79.7 %shard_map.30 = (f32[1024,512]{1,0:T(8,128)}, f32[4,128,256]{2,1,0:T(8,128)}) custom-call(f32[4096,512]{1,0:T(8,128)} %get-tuple-element.21.sy_ref, f32[6,4,4,128,128]{4,3,2,1,0:T(8,128)} %get-tuple-element.22.w_ref, f32[4,8,128,256]{3,2,1,0:T(8,128)} %get-tuple-element.23.c3_ref), custom_call_target="tpu_custom_call" | custom-call | flops 1 | bytes 1024 | tf_op jit(solution)/shard_map/pallas_call | solution.py:711
  431.1 79.5 %shard_map.31 = f32[1024,512]{1,0:T(8,128)} custom-call(f32[1024,512]{1,0:T(8,128)} %get-tuple-element.24.x_ref, f32[4,128,256]{2,1,0:T(8,128)} %get-tuple-element.25.own_ref, f32[4,512,512]{2,1,0:T(8,128)} %get-tuple-element.26.re_ref, f32[4,512,512]{2,1,0:T(8,128)} %get-tuple-element.27.rd_ref, f32[4,512,512]{2,1,0:T(8,128)} %get-tuple-element.28.ro_ref), custom_call_target="tpu_custom_call" | custom-call | flops 1 | bytes 1024 | tf_op jit(solution)/shard_map/pallas_call | solution.py:711
  510.7 4.4 select_select_fusion
  (6 shorter events, 0.0 us)

commit v3 on v2

--- a/solution.py
+++ b/solution.py
@@ -175,14 +175,14 @@
         done(*a)
         a = both(z, a_all, on_z)
         done(*b)
-        b = both(ALL, c_all, on_y, y)
+        b = both(ALL, c_all, on_y, y) if count > first + thin else ()
         if thin:
             b += both(front, t_all, on_y, y)
         yield
         done(*a)
         a = both(z_m, a_0, on_z, None, z_p, a_1)
         done(*b)
-        b = both(ALL, c_0, on_y, y_m, ALL, c_1, y_p)
+        b = both(ALL, c_0, on_y, y_m, ALL, c_1, y_p) if count > first + thin else ()
         if thin:
             b += both(front, t_0, on_y, y_m, front, t_1, y_p)
         yield
@@ -362,7 +362,7 @@
     run(chain(g[1], g[0], g[3], g[3]))
     pair.wait_recv()
 
-    order = iter([2, 2, 3, 1, 3, 2, 1, 2, 0, 1, 0, 1, 0, 0])
+    order = iter([2, 2, 3, 1, 3, 2, 1, 2, 0, 1, 0, 1])
     stores = []
 
     def tick():
@@ -412,17 +412,12 @@
     tick()
     tick()
     s1 = begin(1)
-    run(s3, s2)
+    run(chain(s3, s1, s2, s1))
     for copy in sent:
         copy.wait_recv()
     columns = net.gather_x(col_ref)
-    step(columns)
-    run(s1, columns)
     flip = net.swap(a_ref, b_ref, False)
-    step(flip)
-    for _ in range(U):
-        tick()
-    step(flip)
+    run(chain(columns, s2, s1, g[0], columns, s1, flip, columns, columns, g[0], flip))
     keep(0)
     for copy in stores:
         copy.wait()
@@ -440,8 +435,8 @@
         copy.start()
         return copy
 
+    load_a = [local(lr_ref.at[0:2, OFF[u] + B:OFF[u] + Q], la.at[:, B * u:B * (u + 1)]) for u in GROUPS]
     load_0 = [local(lr_ref.at[:, group(0)], l0), local(bar_ref.at[:, 0:B], bv)]
-    load_a = [local(lr_ref.at[0:2, OFF[u] + B:OFF[u] + Q], la.at[:, B * u:B * (u + 1)]) for u in GROUPS]
     load_b = [local(lr_ref.at[:, OFF[u] + Q:OFF[u] + H], lb.at[:, B * u:B * (u + 2)]) for u in (0, 2)]
     load_c = local(lr_ref.at[:, OFF[1] + Q:OFF[2]], l1)
     net.barrier(*[peer for peer, _ in net.line() + net.plane()])
@@ -462,18 +457,13 @@
         re[z, B * u:B * (u + 1), at(B * y)] = wc_ref[u, r]
     diag = net.gather_zy(re, 0, H, Q)
     step(diag)
-    for u in range(1, U):
-        for h in range(2):
-            for v in range(u + 1):
-                own[v, B * (2 * u + h):B * (2 * u + h + 1), :] = block(a, h, u, v)
-    places = [local(own.at[v, Q * (v + 1):], sy_ref.at[K * v + Q * (v + 1):K * (v + 1), at(B * y)]) for v in range(U - 1)]
-    for place in places:
-        place.wait()
     early = [net.gather_y(sy_ref, K * v + Q * (v + 1), K - Q * (v + 1)) for v in range(U - 1)]
     late = net.gather_y(sy_ref, 3 * K, K)
     e0, e1, e2 = early
     half = pl.ds(2 * net.core, 2)
-    step(e0)
+
+    def odd(rows):
+        return jnp.concatenate([rd[0, rows], rd[1, rows], re[2, rows], re[3, rows]], axis=1)
 
     for u in GROUPS:
         load_a[u].wait()
@@ -481,10 +471,18 @@
         x1[u, r] = mm(wide(la, slice(B * u, B * (u + 1)), (0, 1)), cd[u, 0:R].reshape(K, B))
     strips = net.gather_x(x1)
     flip = net.swap(b, d, True)
-    run(chain(strips, diag, strips, diag, flip))
+    run(chain(strips, diag, diag, flip))
+    for u in range(1, U):
+        for h in range(2):
+            for v in range(u + 1):
+                own[v, B * (2 * u + h):B * (2 * u + h + 1), :] = block(a, h, u, v)
+    places = [local(own.at[v, Q * (v + 1):], sy_ref.at[K * v + Q * (v + 1):K * (v + 1), at(B * y)]) for v in range(U - 1)]
+    step(strips)
     for load in load_0:
         load.wait()
     inner(net, 0, 0, l0, 0, bv, terms)
+    for place in places:
+        place.wait()
 
     def put(k, val):
         s_top[k] = val
@@ -505,7 +503,7 @@
         w = jnp.where(low, w, wc_ref[u, r])
         cd[u, R + r] = w
         rd[z, B * u:B * (u + 1), at(B * y)] = w
-    rows = net.gather_zy(rd, 0, H, Q)
+    rows = net.gather_zy(rd, 0, H, B, H - B)
     step(rows)
     run(net.gather_x(cd, first=R), behind=[chain(rows, e1, rows, e0)])
     stores.append(local(cd.at[:, pl.ds(U * z, U)], w_ref.at[0:U, z]))
@@ -517,12 +515,12 @@
     for q in range(2):
         load_b[q].wait()
         x2[2 * q:2 * q + 2, r] = mm(wide(lb, slice(Q * q, Q * (q + 1))), cd[2 * q].reshape(N, B)).reshape(2, B, B)
-    run(net.gather_x(x2), behind=[chain(e1, rows, e2, e1)])
+    run(net.gather_x(x2), behind=[chain(e1, rows, e2, e1, e0)])
     run(rows)
     stores.append(local(rd, row_d))
     for q in range(2):
         at_u = slice(B * (2 * q + 1), B * (2 * q + 2))
-        tops = (mm(wide(re, at_u, (0, 1)), x2[2 * q].reshape(K, B)), mm(wide(rd, at_u), x2[2 * q:2 * q + 2].reshape(N, B)))
+        tops = (mm(wide(re, at_u, (0, 1)), x2[2 * q].reshape(K, B)), mm(odd(at_u), x2[2 * q:2 * q + 2].reshape(N, B)))
         for i, w in enumerate(tops):
             co[2 * q + i, r] = -w
             ro[z, B * (2 * q + i):B * (2 * q + i + 1), at(B * y)] = -w
@@ -569,7 +567,7 @@
         if i % 2 == 0:
             w = mm(wide(re, at_u, (0, 1)), x3[i].reshape(K, Q))
         else:
-            w = mm(wide(rd, at_u), x3[i - 1:i + 1].reshape(N, Q))
+            w = mm(odd(at_u), x3[i - 1:i + 1].reshape(N, Q))
         if i >= 2:
             w = w + mm(wide(ro, slice(B * i, B * (i + 1))), x3[0:2].reshape(N, Q))
         c3[i, r] = -w
@@ -654,7 +652,8 @@
                     wr, terms, acc, fwd, end, dma_sems, send_sems, recv_sems):
     net = Net(send_sems, recv_sems)
     loads = [[(re_ref.at[0:2, B * u:B * (u + 1)], wr.at[0:2, OFF[u]:OFF[u] + B]),
-              (rd_ref.at[:, B * u:B * (u + 1)], wr.at[:, OFF[u] + B:OFF[u] + Q])] for u in GROUPS]
+              *[(ref.at[zs, B * u:B * (u + 1)], wr.at[zs, OFF[u] + B:OFF[u] + Q])
+                for ref, zs in ((rd_ref, slice(0, 2)), (re_ref, slice(2, U)))]] for u in GROUPS]
     loads[2] += [(ro_ref.at[:, Q:], wr.at[:, OFF[2] + Q:OFF[3]])]
     loads[0] += [(ro_ref.at[:, :Q], wr.at[:, Q:H])]
     sems = iter(range(16))
@@ -739,7 +738,7 @@
         out, = call(
             gradient_kernel, 3, 1, (m, own, row_e, row_d, row_o), [VM] * 2 + [HB] * 3, ((K, H),), [VM],
             (panel, (U, 2, K, H), (U, K, H), (2, H, H), (U, H, H)), ((16,), (64,), (64,)))
-        row, col = lax.broadcasted_iota(jnp.int32, out.shape, 0), lax.broadcasted_iota(jnp.int32, out.shape, 1)
+        row, col = lax.broadcasted_iota(jnp.int32, (K, 1), 0), lax.broadcasted_iota(jnp.int32, (1, H), 1)
         row_all = (row // B * R + lax.axis_index('row')) * B + row % B
         col_all = (col // B * 2 * R + lax.axis_index('col')) * B + col % B
         return jnp.where(row_all > col_all, out, jnp.where(row_all == col_all, 0.5 * out, 0.0))

time: 525 us -> 514 us (0.979)
  Pallas kernels: 511 us -> 501 us
    pallas_call x4, Pallas kernels: 511 us -> 501 us  [call(): pl.pallas_call(kernel, out_shape=[jax.ShapeDtypeStruct(s, jnp.float32) fo...]
where the time goes in v3:
time: 514 us; the launch traced here: 505 us
  Pallas kernels  501 us (97%)
    pallas_call x4, Pallas kernels, call(): pl.pallas_call(kernel, out_shape=[jax.ShapeDtypeStruct(s, jnp.float32) fo...  501 us

profile of v3, /device:TPU:1, one launch (start us, length us, event | category | flops | bytes accessed | tf_op | source)
XLA Modules:
  0.0 505.1 jit_solution(7037863880845723972)
XLA Ops:
  0.0 152.4 %shard_map.28 = (f32[4,2560,512]{2,1,0:T(8,128)}, f32[4,8,128,128]{3,2,1,0:T(8,128)}, f32[2,8,144,128]{3,2,1,0:T(8,128)}, f32[2,8,144,128]{3,2,1,0:T(8,128)}) custom-call(f32[1024,512]{1,0:T(8,128)} %l_ref.1, f32[1024,512]{1,0:T(8,128)} %bar_ref.3), custom_call_target="tpu_custom_call" | custom-call | flops 1 | bytes 1024 | tf_op jit(solution)/shard_map/pallas_call | solution.py:710
  152.5 189.2 %shard_map.29 = (f32[4096,512]{1,0:T(8,128)}, f32[6,4,4,128,128]{4,3,2,1,0:T(8,128)}, f32[4,512,512]{2,1,0:T(8,128)}, f32[4,512,512]{2,1,0:T(8,128)}, f32[4,512,...) custom-call(f32[4,2560,512]{2,1,0:T(8,128)} %get-tuple-element.17.lr_ref, f32[1024,512]{1,0:T(8,128)} %bar_ref.3, ...), custom_call_target="tpu_custom_call" | custom-call | flops 1 | bytes 1024 | tf_op jit(solution)/shard_map/pallas_call | solution.py:710
  341.7 82.3 %shard_map.30 = (f32[1024,512]{1,0:T(8,128)}, f32[4,128,256]{2,1,0:T(8,128)}) custom-call(f32[4096,512]{1,0:T(8,128)} %get-tuple-element.21.sy_ref, f32[6,4,4,128,128]{4,3,2,1,0:T(8,128)} %get-tuple-element.22.w_ref, f32[4,8,128,256]{3,2,1,0:T(8,128)} %get-tuple-element.23.c3_ref), custom_call_target="tpu_custom_call" | custom-call | flops 1 | bytes 1024 | tf_op jit(solution)/shard_map/pallas_call | solution.py:710
  424.0 77.4 %shard_map.31 = f32[1024,512]{1,0:T(8,128)} custom-call(f32[1024,512]{1,0:T(8,128)} %get-tuple-element.24.x_ref, f32[4,128,256]{2,1,0:T(8,128)} %get-tuple-element.25.own_ref, f32[4,512,512]{2,1,0:T(8,128)} %get-tuple-element.26.re_ref, f32[4,512,512]{2,1,0:T(8,128)} %get-tuple-element.27.rd_ref, f32[4,512,512]{2,1,0:T(8,128)} %get-tuple-element.28.ro_ref), custom_call_target="tpu_custom_call" | custom-call | flops 1 | bytes 1024 | tf_op jit(solution)/shard_map/pallas_call | solution.py:710
  501.4 3.3 select_select_fusion
  (2 shorter events, 0.0 us)

commit v4 on v3

--- a/solution.py
+++ b/solution.py
@@ -508,6 +508,7 @@
     run(net.gather_x(cd, first=R), behind=[chain(rows, e1, rows, e0)])
     stores.append(local(cd.at[:, pl.ds(U * z, U)], w_ref.at[0:U, z]))
     out = net.spread_z((lambda k: cd.at[:, pl.ds(U * k + 2 * net.core, 2)], lambda k: w_ref.at[0:U, k, half]))
+    step(out)
     step(flip)
     flip = net.swap(d, back, False)
     step(flip)
@@ -526,8 +527,21 @@
             ro[z, B * (2 * q + i):B * (2 * q + i + 1), at(B * y)] = -w
     rows = net.gather_zy(ro, 0, H, Q)
     step(rows)
-    step(out)
     strips = net.gather_x(co)
+    step(strips)
+
+    run(strips, behind=[chain(rows, e2, rows, out)])
+    parts = []
+    for q in range(2):
+        stores.append(local(co.at[2 * q + z // 2, pl.ds(U * lax.rem(z, 2), U)], w_ref.at[U + q, z]))
+        parts.append((lambda k, q=q: co.at[2 * q + k // 2, pl.ds(U * lax.rem(k, 2) + 2 * net.core, 2)],
+                      lambda k, q=q: w_ref.at[U + q, k, half]))
+    out_o = net.spread_z(*parts)
+
+    load_c.wait()
+    x3[:, r] = mm(wide(l1, ALL), jnp.concatenate([co[0:2].reshape(N, B), cd[1].reshape(N, B)], 1)).reshape(U, B, Q)
+    x3[:, r, :, :B] = x3[:, r, :, :B] + mm(wide(l0, slice(H, K)), cd[0].reshape(N, B)).reshape(U, B, B)
+    strips = net.gather_x(x3)
     step(strips)
 
     step(flip)
@@ -543,22 +557,11 @@
                 val = (block(back, s, u, v) if u else top_back[s]).T
                 own[u, at_t, :] = own[u, at_t, :] + val if u == v else val
     places = [local(own.at[v, 0:Q * (v + 1)], sy_ref.at[K * v:K * v + Q * (v + 1), at(B * y)]) for v in GROUPS]
-    run(strips, behind=[chain(rows, e2, rows, out)])
+    run(strips, behind=[chain(rows, out, e2)])
+    run(rows)
     for place in places:
         place.wait()
     step(late)
-    parts = []
-    for q in range(2):
-        stores.append(local(co.at[2 * q + z // 2, pl.ds(U * lax.rem(z, 2), U)], w_ref.at[U + q, z]))
-        parts.append((lambda k, q=q: co.at[2 * q + k // 2, pl.ds(U * lax.rem(k, 2) + 2 * net.core, 2)],
-                      lambda k, q=q: w_ref.at[U + q, k, half]))
-    out_o = net.spread_z(*parts)
-
-    load_c.wait()
-    x3[:, r] = mm(wide(l1, ALL), jnp.concatenate([co[0:2].reshape(N, B), cd[1].reshape(N, B)], 1)).reshape(U, B, Q)
-    x3[:, r, :, :B] = x3[:, r, :, :B] + mm(wide(l0, slice(H, K)), cd[0].reshape(N, B)).reshape(U, B, B)
-    run(net.gather_x(x3), behind=[chain(rows, late, out, e2)])
-    run(rows)
     step(out_o)
     stores.append(local(ro, row_o))
     for i in GROUPS:

time: 514 us -> 502 us (0.977)
  Pallas kernels: 501 us -> 489 us
    pallas_call x4, Pallas kernels: 501 us -> 489 us  [call(): pl.pallas_call(kernel, out_shape=[jax.ShapeDtypeStruct(s, jnp.float32) fo...]
where the time goes in v4:
time: 502 us; the launch traced here: 493 us
  Pallas kernels  489 us (97%)
    pallas_call x4, Pallas kernels, call(): pl.pallas_call(kernel, out_shape=[jax.ShapeDtypeStruct(s, jnp.float32) fo...  489 us

profile of v4, /device:TPU:1, one launch (start us, length us, event | category | flops | bytes accessed | tf_op | source)
XLA Modules:
  0.0 492.9 jit_solution(1044349201887188605)
XLA Ops:
  0.0 152.4 %shard_map.28 = (f32[4,2560,512]{2,1,0:T(8,128)}, f32[4,8,128,128]{3,2,1,0:T(8,128)}, f32[2,8,144,128]{3,2,1,0:T(8,128)}, f32[2,8,144,128]{3,2,1,0:T(8,128)}) custom-call(f32[1024,512]{1,0:T(8,128)} %l_ref.1, f32[1024,512]{1,0:T(8,128)} %bar_ref.3), custom_call_target="tpu_custom_call" | custom-call | flops 1 | bytes 1024 | tf_op jit(solution)/shard_map/pallas_call | solution.py:713
  152.5 176.3 %shard_map.29 = (f32[4096,512]{1,0:T(8,128)}, f32[6,4,4,128,128]{4,3,2,1,0:T(8,128)}, f32[4,512,512]{2,1,0:T(8,128)}, f32[4,512,512]{2,1,0:T(8,128)}, f32[4,512,...) custom-call(f32[4,2560,512]{2,1,0:T(8,128)} %get-tuple-element.17.lr_ref, f32[1024,512]{1,0:T(8,128)} %bar_ref.3, ...), custom_call_target="tpu_custom_call" | custom-call | flops 1 | bytes 1024 | tf_op jit(solution)/shard_map/pallas_call | solution.py:713
  328.7 82.2 %shard_map.30 = (f32[1024,512]{1,0:T(8,128)}, f32[4,128,256]{2,1,0:T(8,128)}) custom-call(f32[4096,512]{1,0:T(8,128)} %get-tuple-element.21.sy_ref, f32[6,4,4,128,128]{4,3,2,1,0:T(8,128)} %get-tuple-element.22.w_ref, f32[4,8,128,256]{3,2,1,0:T(8,128)} %get-tuple-element.23.c3_ref), custom_call_target="tpu_custom_call" | custom-call | flops 1 | bytes 1024 | tf_op jit(solution)/shard_map/pallas_call | solution.py:713
  410.9 78.2 %shard_map.31 = f32[1024,512]{1,0:T(8,128)} custom-call(f32[1024,512]{1,0:T(8,128)} %get-tuple-element.24.x_ref, f32[4,128,256]{2,1,0:T(8,128)} %get-tuple-element.25.own_ref, f32[4,512,512]{2,1,0:T(8,128)} %get-tuple-element.26.re_ref, f32[4,512,512]{2,1,0:T(8,128)} %get-tuple-element.27.rd_ref, f32[4,512,512]{2,1,0:T(8,128)} %get-tuple-element.28.ro_ref), custom_call_target="tpu_custom_call" | custom-call | flops 1 | bytes 1024 | tf_op jit(solution)/shard_map/pallas_call | solution.py:713
  489.2 3.3 select_select_fusion
  (2 shorter events, 0.0 us)

commit v5 on v4

--- a/solution.py
+++ b/solution.py
@@ -85,7 +85,7 @@
         sem = pltpu.get_barrier_semaphore()
         for peer in peers:
             pl.semaphore_signal(sem, inc=1, device_id=peer, device_id_type=MESH)
-        pl.semaphore_wait(sem, len(peers))
+        return lambda: pl.semaphore_wait(sem, len(peers))
 
     def line(self):
         places = [(mod4(self.x + d // 2), lax.rem(self.core + d, 2)) for d in range(1, R)]
@@ -343,7 +343,10 @@
     others = [net.device(y=mod4(y + d)) for d in ways]
     for u in GROUPS:
         lv[2:, OFF[u]:OFF[u] + B] = jnp.zeros((2, B, H), jnp.float32)
-    net.barrier(*[peer for peer, _ in net.line()], *others, *net.zy[2:])
+    ready = net.barrier(*[peer for peer, _ in net.line()], *others, *net.zy[2:])
+    for u in GROUPS:
+        lv[z, group(u), at(B * y)] = l_ref[Q * u:, B * u:B * (u + 1)]
+    ready()
 
     strip = at(B * (U * zz + y))
 
@@ -352,8 +355,6 @@
 
     sent = [net.copy(l_ref.at[own(mod4(y + d))], other, lss.at[r, :, strip]) for d, other in zip(ways, others)]
     lss[r, :, strip] = l_ref[own(y)]
-    for u in GROUPS:
-        lv[z, group(u), at(B * y)] = l_ref[Q * u:, B * u:B * (u + 1)]
     g = [net.gather_zy(lv, OFF[u], K - Q * u, (K - Q * u - 96) // 2, B) for u in GROUPS]
     run(chain(g[3], g[2]))
     for copy in sent:
@@ -424,8 +425,8 @@
     net.drain()
 
 
-def levels_kernel(lr_ref, bar_ref, wc_ref, a, b, sy_ref, w_ref, row_e, row_d, row_o, col_3,
-                  own, d, back, s_top, top_back, la, lb, l0, l1, bv, cd, re, rd, co, ro, c3, x1, x2, x3, terms, acc, fwd, end, dma_sems, send_sems, recv_sems, t_send, t_recv):
+def levels_kernel(lr_ref, bar_ref, wc_ref, a_ref, b_ref, sy_ref, w_ref, row_e, row_d, row_o, col_3,
+                  own, a, b, d, back, s_top, top_back, la, lb, l0, l1, bv, cd, re, rd, co, ro, c3, x1, x2, x3, terms, acc, fwd, end, dma_sems, send_sems, recv_sems, t_send, t_recv):
     net = Net(send_sems, recv_sems)
     r, c, y, z = net.r, net.c, net.y, net.z
     sems = iter(range(32))
@@ -437,9 +438,10 @@
 
     load_a = [local(lr_ref.at[0:2, OFF[u] + B:OFF[u] + Q], la.at[:, B * u:B * (u + 1)]) for u in GROUPS]
     load_0 = [local(lr_ref.at[:, group(0)], l0), local(bar_ref.at[:, 0:B], bv)]
+    load_s = [local(a_ref, a), local(b_ref, b)]
     load_b = [local(lr_ref.at[:, OFF[u] + Q:OFF[u] + H], lb.at[:, B * u:B * (u + 2)]) for u in (0, 2)]
     load_c = local(lr_ref.at[:, OFF[1] + Q:OFF[2]], l1)
-    net.barrier(*[peer for peer, _ in net.line() + net.plane()])
+    ready = net.barrier(*[peer for peer, _ in net.line() + net.plane()])
     half_c, row_c = c // R, lax.rem(c, R)
     swap = [{'row': row_c, 'col': r + R * h} for h in range(2)]
     away = [(row_c != r) | (half_c != h) for h in range(2)]
@@ -455,6 +457,9 @@
     stores = []
     for u in GROUPS:
         re[z, B * u:B * (u + 1), at(B * y)] = wc_ref[u, r]
+    for u in GROUPS:
+        cd[u, 0:R] = jnp.where(low, wc_ref[u], 0.0)
+    ready()
     diag = net.gather_zy(re, 0, H, Q)
     step(diag)
     early = [net.gather_y(sy_ref, K * v + Q * (v + 1), K - Q * (v + 1)) for v in range(U - 1)]
@@ -467,10 +472,11 @@
 
     for u in GROUPS:
         load_a[u].wait()
-        cd[u, 0:R] = jnp.where(low, wc_ref[u], 0.0)
         x1[u, r] = mm(wide(la, slice(B * u, B * (u + 1)), (0, 1)), cd[u, 0:R].reshape(K, B))
     strips = net.gather_x(x1)
     flip = net.swap(b, d, True)
+    for load in load_s:
+        load.wait()
     run(chain(strips, diag, diag, flip))
     for u in range(1, U):
         for h in range(2):
@@ -505,7 +511,7 @@
         rd[z, B * u:B * (u + 1), at(B * y)] = w
     rows = net.gather_zy(rd, 0, H, B, H - B)
     step(rows)
-    run(net.gather_x(cd, first=R), behind=[chain(rows, e1, rows, e0)])
+    run(net.gather_x(cd, first=R), behind=[chain(rows, rows, e1, e0)])
     stores.append(local(cd.at[:, pl.ds(U * z, U)], w_ref.at[0:U, z]))
     out = net.spread_z((lambda k: cd.at[:, pl.ds(U * k + 2 * net.core, 2)], lambda k: w_ref.at[0:U, k, half]))
     step(out)
@@ -597,13 +603,14 @@
         load.start()
     for load in loads[:U]:
         load.wait()
-    net.barrier(*net.zy, net.far_z, net.partner)
+    ready = net.barrier(*net.zy, net.far_z, net.partner)
     half = pl.ds(2 * net.core, 2)
     parts = []
     for v in range(2):
         wide_w[v, z] = c3[2 * v + z // 2, pl.ds(U * lax.rem(z, 2), U)]
         parts.append((lambda k, v=v: c3.at[2 * v + k // 2, pl.ds(U * lax.rem(k, 2) + 2 * net.core, 2)],
                       lambda k, v=v: wide_w.at[v, k, half]))
+    ready()
     out = net.spread_z(*parts)
     step(out)
     own_ref[...] = c3[:, net.r]
@@ -664,10 +671,11 @@
     for some in loads[::-1]:
         for load in some:
             load.start()
-    net.barrier(net.right, net.left, net.partner, *net.zy)
+    ready = net.barrier(net.right, net.left, net.partner, *net.zy)
     for i in GROUPS:
         for k, top in enumerate((H, OFF[1] + Q)):
             wr[net.z, top + B * i:top + B * (i + 1), at(B * net.y)] = own_ref[i, :, B * k:B * (k + 1)]
+    ready()
     rows_0, rows_1 = net.gather_zy(wr, H, H, Q), net.gather_zy(wr, OFF[1] + Q, H, Q)
     step(rows_1)
     step(rows_0)
@@ -730,9 +738,9 @@
             (panel, (R, B, K), (R, B, K), (U, Q, Q), (U, 2, ROWS, B), (U, ROWS, B), (2, ROWS // 2, B), (U, ROWS // 2, B)),
             ((U,), (144,), (144,)))
         sy, w, row_e, row_d, row_o, col_3 = call(
-            levels_kernel, 1, 1, (lr, bar, wc, a, b), [HB, HB, VM, VM, VM],
+            levels_kernel, 1, 1, (lr, bar, wc, a, b), [HB, HB, VM, HB, HB],
             ((U * K, H), (6, U, U, B, B), rows, rows, rows, wide_col), [HB] * 6,
-            ((U, K, B), cut, cut, (2, B, B), (2, B, B), (2, H, H), rows, (U, K, H), rows, (K, B), (U, 2 * R, B, B), rows, rows, column, rows,
+            ((U, K, B), cut, cut, cut, cut, (2, B, B), (2, B, B), (2, H, H), rows, (U, K, H), rows, (K, B), (U, 2 * R, B, B), rows, rows, column, rows,
              wide_col, column, column, wide_col, (U, 2, Q, B), (U, Q, B), (2, B, B), (U, B, B)),
             ((48,), (208,), (208,), (2,), (2,)))
         m, own = call(

time: 502 us -> 500 us (level)
  no operation moved by 1% of the time
where the time goes in v5:
time: 500 us; the launch traced here: 490 us
  Pallas kernels  487 us (97%)
    pallas_call x4, Pallas kernels, call(): pl.pallas_call(kernel, out_shape=[jax.ShapeDtypeStruct(s, jnp.float32) fo...  487 us

profile of v5, /device:TPU:1, one launch (start us, length us, event | category | flops | bytes accessed | tf_op | source)
XLA Modules:
  0.0 490.4 jit_solution(14578763324975090821)
XLA Ops:
  0.0 152.3 %shard_map.28 = (f32[4,2560,512]{2,1,0:T(8,128)}, f32[4,8,128,128]{3,2,1,0:T(8,128)}, f32[2,8,144,128]{3,2,1,0:T(8,128)}, f32[2,8,144,128]{3,2,1,0:T(8,128)}) custom-call(f32[1024,512]{1,0:T(8,128)} %l_ref.1, f32[1024,512]{1,0:T(8,128)} %bar_ref.3), custom_call_target="tpu_custom_call" | custom-call | flops 1 | bytes 1024 | tf_op jit(solution)/shard_map/pallas_call | solution.py:721
  152.3 175.1 %shard_map.29 = (f32[4096,512]{1,0:T(8,128)}, f32[6,4,4,128,128]{4,3,2,1,0:T(8,128)}, f32[4,512,512]{2,1,0:T(8,128)}, f32[4,512,512]{2,1,0:T(8,128)}, f32[4,512,...) custom-call(f32[4,2560,512]{2,1,0:T(8,128)} %get-tuple-element.17.lr_ref, f32[1024,512]{1,0:T(8,128)} %bar_ref.3, ...), custom_call_target="tpu_custom_call" | custom-call | flops 1 | bytes 1024 | tf_op jit(solution)/shard_map/pallas_call | solution.py:721
  327.4 83.0 %shard_map.30 = (f32[1024,512]{1,0:T(8,128)}, f32[4,128,256]{2,1,0:T(8,128)}) custom-call(f32[4096,512]{1,0:T(8,128)} %get-tuple-element.21.sy_ref, f32[6,4,4,128,128]{4,3,2,1,0:T(8,128)} %get-tuple-element.22.w_ref, f32[4,8,128,256]{3,2,1,0:T(8,128)} %get-tuple-element.23.c3_ref), custom_call_target="tpu_custom_call" | custom-call | flops 1 | bytes 1024 | tf_op jit(solution)/shard_map/pallas_call | solution.py:721
  410.4 76.2 %shard_map.31 = f32[1024,512]{1,0:T(8,128)} custom-call(f32[1024,512]{1,0:T(8,128)} %get-tuple-element.24.x_ref, f32[4,128,256]{2,1,0:T(8,128)} %get-tuple-element.25.own_ref, f32[4,512,512]{2,1,0:T(8,128)} %get-tuple-element.26.re_ref, f32[4,512,512]{2,1,0:T(8,128)} %get-tuple-element.27.rd_ref, f32[4,512,512]{2,1,0:T(8,128)} %get-tuple-element.28.ro_ref), custom_call_target="tpu_custom_call" | custom-call | flops 1 | bytes 1024 | tf_op jit(solution)/shard_map/pallas_call | solution.py:721
  486.7 3.3 select_select_fusion
  (2 shorter events, 0.0 us)

commit v6 on v5

--- a/solution.py
+++ b/solution.py
@@ -335,9 +335,11 @@
     lax.fori_loop(0, R, two, 0)
 
 
-def front_kernel(l_ref, bar_ref, lr_ref, col_ref, a_ref, b_ref, lv, lss, wss, tmp, terms, acc, fwd, end, dma_sems, send_sems, recv_sems):
+def front_kernel(l_ref, bar_ref, lr_ref, col_ref, a_ref, b_ref, bar, lv, lss, wss, tmp, terms, acc, fwd, end, dma_sems, send_sems, recv_sems):
     net = Net(send_sems, recv_sems)
     r, c, y, z, core = net.r, net.c, net.y, net.z, net.core
+    load = pltpu.make_async_copy(bar_ref, bar, dma_sems.at[U])
+    load.start()
     half, zz = z // 2, lax.rem(z, 2)
     ways = (1, 2, 3)
     others = [net.device(y=mod4(y + d)) for d in ways]
@@ -377,7 +379,7 @@
 
     def begin(u):
         start = ROWS - Q * (u + 1) * (u + 2) // 2
-        inner(net, u, start, lv, OFF[u], bar_ref, terms)
+        inner(net, u, start, lv, OFF[u], bar, terms)
 
         def put(k, val):
             v, h = k // 2, k % 2
@@ -395,6 +397,7 @@
     for _ in range(2):
         tick()
     step(strips)
+    load.wait()
     s3 = begin(3)
     run(strips)
     step(s3)
@@ -734,9 +737,9 @@
         panel, rows, column = (U, ROWS, H), (U, H, H), (U, R, B, B)
         wide_col, cut = (U, R, B, Q), (2, R, (ROWS - Q) // (2 * R), B)
         lr, wc, a, b = call(
-            front_kernel, 0, 1, (fac, bar), [VM] * 2, (panel, column, cut, cut), [HB] + [VM] * 3,
-            (panel, (R, B, K), (R, B, K), (U, Q, Q), (U, 2, ROWS, B), (U, ROWS, B), (2, ROWS // 2, B), (U, ROWS // 2, B)),
-            ((U,), (144,), (144,)))
+            front_kernel, 0, 1, (fac, bar), [VM, HB], (panel, column, cut, cut), [HB] + [VM] * 3,
+            ((K, H), panel, (R, B, K), (R, B, K), (U, Q, Q), (U, 2, ROWS, B), (U, ROWS, B), (2, ROWS // 2, B), (U, ROWS // 2, B)),
+            ((U + 1,), (144,), (144,)))
         sy, w, row_e, row_d, row_o, col_3 = call(
             levels_kernel, 1, 1, (lr, bar, wc, a, b), [HB, HB, VM, HB, HB],
             ((U * K, H), (6, U, U, B, B), rows, rows, rows, wide_col), [HB] * 6,

time: 500 us -> 498 us (level)
  no operation moved by 1% of the time
where the time goes in v6:
time: 498 us; the launch traced here: 489 us
  Pallas kernels  485 us (97%)
    pallas_call x4, Pallas kernels, call(): pl.pallas_call(kernel, out_shape=[jax.ShapeDtypeStruct(s, jnp.float32) fo...  485 us

profile of v6, /device:TPU:1, one launch (start us, length us, event | category | flops | bytes accessed | tf_op | source)
XLA Modules:
  0.0 489.1 jit_solution(8821889894267973752)
XLA Ops:
  0.0 151.6 %shard_map.28 = (f32[4,2560,512]{2,1,0:T(8,128)}, f32[4,8,128,128]{3,2,1,0:T(8,128)}, f32[2,8,144,128]{3,2,1,0:T(8,128)}, f32[2,8,144,128]{3,2,1,0:T(8,128)}) custom-call(f32[1024,512]{1,0:T(8,128)} %l_ref.1, f32[1024,512]{1,0:T(8,128)} %bar_ref.3), custom_call_target="tpu_custom_call" | custom-call | flops 1 | bytes 1024 | tf_op jit(solution)/shard_map/pallas_call | solution.py:724
  151.6 175.0 %shard_map.29 = (f32[4096,512]{1,0:T(8,128)}, f32[6,4,4,128,128]{4,3,2,1,0:T(8,128)}, f32[4,512,512]{2,1,0:T(8,128)}, f32[4,512,512]{2,1,0:T(8,128)}, f32[4,512,...) custom-call(f32[4,2560,512]{2,1,0:T(8,128)} %get-tuple-element.17.lr_ref, f32[1024,512]{1,0:T(8,128)} %bar_ref.3, ...), custom_call_target="tpu_custom_call" | custom-call | flops 1 | bytes 1024 | tf_op jit(solution)/shard_map/pallas_call | solution.py:724
  326.6 82.7 %shard_map.30 = (f32[1024,512]{1,0:T(8,128)}, f32[4,128,256]{2,1,0:T(8,128)}) custom-call(f32[4096,512]{1,0:T(8,128)} %get-tuple-element.21.sy_ref, f32[6,4,4,128,128]{4,3,2,1,0:T(8,128)} %get-tuple-element.22.w_ref, f32[4,8,128,256]{3,2,1,0:T(8,128)} %get-tuple-element.23.c3_ref), custom_call_target="tpu_custom_call" | custom-call | flops 1 | bytes 1024 | tf_op jit(solution)/shard_map/pallas_call | solution.py:724
  409.3 76.0 %shard_map.31 = f32[1024,512]{1,0:T(8,128)} custom-call(f32[1024,512]{1,0:T(8,128)} %get-tuple-element.24.x_ref, f32[4,128,256]{2,1,0:T(8,128)} %get-tuple-element.25.own_ref, f32[4,512,512]{2,1,0:T(8,128)} %get-tuple-element.26.re_ref, f32[4,512,512]{2,1,0:T(8,128)} %get-tuple-element.27.rd_ref, f32[4,512,512]{2,1,0:T(8,128)} %get-tuple-element.28.ro_ref), custom_call_target="tpu_custom_call" | custom-call | flops 1 | bytes 1024 | tf_op jit(solution)/shard_map/pallas_call | solution.py:724
  485.4 3.3 select_select_fusion
  (2 shorter events, 0.0 us)
